TPU v7x, 32 devices: a whole 2x2x4 slice. The times are simulated.
32 devices in a mesh: ep: 8 (over y, x, core), dp: 4 (over z).
Axes of the slice: x: 2, y: 2, z: 4, core: 2. Of those that a mesh axis runs over, the one named last changes fastest.
Arguments:
- tokens: bfloat16 [64, 7168], P('dp', 'ep'), may hold values from -6 to 6
- norm_gain: float32 [2, 7168], replicated, may hold values from 0.1 to 1.9
- gate_weight: bfloat16 [2, 12, 2048, 7168], P(None, 'dp', 'ep'), may hold values from -0.0625 to 0.0625
- up_weight: bfloat16 [2, 12, 2048, 7168], P(None, 'dp', 'ep'), may hold values from -0.0625 to 0.0625
- down_weight: bfloat16 [2, 12, 7168, 2048], P(None, 'dp', 'ep'), may hold values from -0.125 to 0.125
- replica_plan: int32 [2, 4, 2], replicated, may hold values from 0 to 2
- route_expert: int32 [2, 64, 8], replicated, may hold values from 0 to 11, as said below
- replica_pick: int32 [2, 64, 8], replicated, may hold values from 0 to 2
- combine_num: int32 [2, 64, 8], P(None, 'dp'), may hold values from 1 to 8
Outputs:
- stream_out: bfloat16 [64, 7168], P('dp', 'ep')
- last_update: bfloat16 [64, 7168], P('dp', 'ep')
Inputs may be any that keep to these rules, and one draw needn't show every extreme that they name: `route_expert`: each row of one layer names 8 different experts.
All inputs are finite; a program needn't handle non-finite values.
Results may differ from a plain program's by a relative error of at most 0.011.
Values may be sent and summed in bfloat16 or wider, within the bound.
No kernel may reach another device: no remote copies, remote signals or barrier semaphores. Data moves between devices by JAX's collectives and lax.ppermute only.
A program may use at most 256 MiB of HBM per device.

v0:
```python
import functools

import jax
import jax.numpy as jnp
from jax import lax
from jax.experimental import pallas as pl
from jax.experimental.pallas import tpu as pltpu
from jax.sharding import PartitionSpec as P


epsilon = 1e-06
lanes = 128
widest = 8
bf16 = jnp.bfloat16
f32 = jnp.float32


def routing(plan_ref, route_ref, pick_ref, mask_ref, sizes):
    layers, groups, rows, top, exp_host, rep_host, capacity = sizes
    host = lax.axis_index("dp")
    replicas = exp_host + rep_host
    tokens = groups * rows
    slots = -(-groups * replicas // 8) * 8
    slot_i = lax.broadcasted_iota(jnp.int32, (slots, 1), 0)
    from_i = lax.broadcasted_iota(jnp.int32, (tokens, lanes), 0)
    to_i = lax.broadcasted_iota(jnp.int32, (tokens, lanes), 1)
    earlier = jnp.where((from_i // rows == to_i // rows) & (from_i < to_i), 1.0, 0.0).astype(bf16)[:, :tokens]
    swap = jnp.where((from_i // rows == (to_i // rows) ^ host) & (from_i % rows == to_i % rows), 1.0, 0.0).astype(bf16)
    for layer in range(layers):
        served = []
        for slot in range(groups * replicas):
            owner, local = divmod(slot, replicas)
            if local < exp_host:
                served.append(owner * exp_host + local)
            else:
                copy = local - exp_host
                served.append(((owner - 1 - copy) % groups) * exp_host + plan_ref[layer, copy, owner])
        table = jnp.full((slots, 1), -1, jnp.int32)
        for slot, expert in enumerate(served):
            table = jnp.where(slot_i == slot, expert, table)
        rank = jnp.zeros((slots, 1), f32)
        count = jnp.zeros((slots, 1), f32)
        for slot, expert in enumerate(served):
            same = jnp.where(table == expert, 1.0, 0.0)
            count = count + same
            rank = rank + jnp.where(slot_i > slot, same, 0.0)
        count = jnp.broadcast_to(jnp.maximum(count, 1.0), (slots, tokens))
        rank = jnp.broadcast_to(rank, (slots, tokens))
        table = jnp.broadcast_to(table, (slots, tokens))
        experts = route_ref[layer]
        picks = pick_ref[layer].astype(f32)
        chosen = []
        for k in range(top):
            pick = picks[k : k + 1, :]
            wanted = pick - count * jnp.floor((pick + 0.5) / count)
            chosen.append(jnp.where((experts[k : k + 1, :] == table) & (rank == wanted), 1.0, 0.0))
        total = functools.reduce(lambda a, b: a + b, chosen)
        before = jnp.dot(total.astype(bf16), earlier, preferred_element_type=f32)
        kept = []
        for k in range(top):
            position = jnp.sum(before * chosen[k], axis=0, keepdims=True)
            before = before + chosen[k]
            kept.append(jnp.where(position < capacity - 0.5, 1.0, 0.0))
        kept = jnp.concatenate(kept, axis=0)
        for j in range(exp_host):
            mask = jnp.where(experts == host * exp_host + j, kept, 0.0)
            mask_ref[layer, j] = jnp.dot(mask.astype(bf16), swap, preferred_element_type=f32)


def setup_kernel(
    _, plan_hbm, route_hbm, pick_hbm, gain_hbm, weight_hbm, mask_ref, gain_ref, weight_ref, plan_ref, route_ref, pick_ref, sems, *, sizes
):
    small = [(plan_hbm, plan_ref), (route_hbm, route_ref), (pick_hbm, pick_ref), (gain_hbm, gain_ref)]
    moves = [pltpu.make_async_copy(src, dst, sems.at[i]) for i, (src, dst) in enumerate(small)]
    moves.append(pltpu.make_async_copy(weight_hbm.at[0], weight_ref, sems.at[len(small)]))
    for move in moves:
        move.start()
    for move in moves[:3]:
        move.wait()
    routing(plan_ref, route_ref, pick_ref, mask_ref, sizes)
    for move in moves[3:]:
        move.wait()


def prefetch_kernel(*refs, layer, count):
    sources, results, sems = refs[-2 * count - 1 : -count - 1], refs[-count - 1 : -1], refs[-1]
    moves = [
        pltpu.make_async_copy(src.at[layer], dst, sems.at[i]) for i, (src, dst) in enumerate(zip(sources, results))
    ]
    for move in moves:
        move.start()
    for move in moves:
        move.wait()


def gate_kernel(mask_ref, num_ref, gain_ref, *refs, layer, top, rows, shards, exp_host, units, width):
    x_refs = refs[:shards]
    gate_ref, up_ref, out_ref, acc_ref = refs[shards:]
    column = lax.axis_index("ep")
    pairs = shards // 2
    pair_width = 2 * width
    full = shards * width
    tokens = x_refs[0].shape[0]
    odd = column % 2 == 1
    squares = jnp.zeros((tokens, 1), f32)
    for m in range(pairs):
        mine = x_refs[2 * m][...].astype(f32)
        other = x_refs[2 * m + 1][...].astype(f32)
        squares = squares + jnp.sum(mine * mine + other * other, axis=1, keepdims=True)
        both = jnp.concatenate([jnp.where(odd, other, mine), jnp.where(odd, mine, other)], axis=1)
        offset = pl.multiple_of(((column // 2) ^ m) * pair_width, lanes)
        gain = gain_ref[layer : layer + 1, pl.ds(offset, pair_width)]
        scaled = (both * gain).astype(bf16)
        for i, weight_ref in enumerate((gate_ref, up_ref)):
            part = lax.dot_general(
                weight_ref[:, :, pl.ds(offset, pair_width)].reshape(exp_host * units, pair_width),
                scaled,
                (((1,), (1,)), ((), ())),
                preferred_element_type=f32,
            )
            if m == 0:
                acc_ref[i, :, :tokens] = part
            else:
                acc_ref[i, :, :tokens] = acc_ref[i, :, :tokens] + part
    inverse = lax.rsqrt(squares / full + epsilon)
    turned = jnp.concatenate([jnp.broadcast_to(inverse, (tokens, lanes)), jnp.zeros((lanes - tokens, lanes), f32)], axis=0).T
    scale = turned[0:1, :]
    blocks = num_ref.shape[0] // rows
    numbers = num_ref[0:rows, :].astype(f32)
    for b in range(1, blocks):
        numbers = numbers + pltpu.roll(num_ref[b * rows : (b + 1) * rows, :].astype(f32), b * rows, 1)
    numbers = numbers[layer * top : (layer + 1) * top, :]
    shares = numbers / jnp.maximum(jnp.sum(numbers, axis=0, keepdims=True), 1.0)
    for j in range(exp_host):
        weight = jnp.sum(mask_ref[layer, j] * shares, axis=0, keepdims=True)
        gate = acc_ref[0, j * units : (j + 1) * units, :] * scale
        up = acc_ref[1, j * units : (j + 1) * units, :] * scale
        hidden = gate / (1.0 + jnp.exp(-gate)) * up * weight
        out_ref[j * tokens : (j + 1) * tokens, :] = hidden.T[:tokens].astype(bf16)


def down_kernel(*refs, layer, shards, exp_host, units, width, tokens):
    h_refs = refs[:shards]
    down_ref, own_ref, send_ref, acc_ref = refs[shards:]
    column = lax.axis_index("ep")
    pairs = shards // 2
    pair_units = 2 * units
    odd = column % 2 == 1
    for m in range(pairs):
        parts = []
        for j in range(exp_host):
            mine = h_refs[2 * m][j * tokens : (j + 1) * tokens, :].astype(f32)
            other = h_refs[2 * m + 1][j * tokens : (j + 1) * tokens, :].astype(f32)
            parts += [jnp.where(odd, other, mine), jnp.where(odd, mine, other)]
        hidden = jnp.concatenate(parts, axis=1).astype(bf16)
        offset = pl.multiple_of(((column // 2) ^ m) * pair_units, lanes)
        weights = jnp.concatenate([down_ref[j, :, pl.ds(offset, pair_units)] for j in range(exp_host)], axis=1)
        part = lax.dot_general(weights, hidden, (((1,), (1,)), ((), ())), preferred_element_type=f32)
        if m == 0:
            acc_ref[:, :tokens] = part
        else:
            acc_ref[:, :tokens] = acc_ref[:, :tokens] + part
    result = acc_ref[...].T[:tokens]
    own_ref[...] = result
    send_ref[...] = result.astype(bf16)


def vmem_spec():
    return pl.BlockSpec(memory_space=pltpu.VMEM)


def hbm_spec():
    return pl.BlockSpec(memory_space=pltpu.HBM)


def any_spec():
    return pl.BlockSpec(memory_space=pl.ANY)


def in_hbm(value):
    return pltpu.with_memory_space_constraint(value, pltpu.HBM)


def prefetch(layer, after, *weights):
    size = sum(w.size // w.shape[0] * w.dtype.itemsize for w in weights)
    return pl.pallas_call(
        functools.partial(prefetch_kernel, layer=layer, count=len(weights)),
        out_shape=tuple(pltpu.VMEM(w.shape[1:], w.dtype) for w in weights),
        in_specs=[any_spec()] + [hbm_spec()] * len(weights),
        out_specs=tuple(vmem_spec() for _ in weights),
        scratch_shapes=[pltpu.SemaphoreType.DMA((len(weights),))],
        compiler_params=pltpu.CompilerParams(vmem_limit_bytes=2**20),
        cost_estimate=pl.CostEstimate(flops=400 * size, bytes_accessed=2 * size, transcendentals=0),
    )(after, *[in_hbm(w) for w in weights])


def xor_permute(value, axis, size, bits):
    return lax.ppermute(value, axis, [(i, i ^ bits) for i in range(size)])


def gather_shards(value, size):
    same = {0: value}
    for k in sorted(range(2, size, 2), reverse=True):
        same[k] = xor_permute(value, "ep", size, k)
    both = {}
    for k, part in same.items():
        both[k] = part
        both[k + 1] = xor_permute(part, "ep", size, 1)
    return [both[k] for k in range(size)]


def fast_device(tokens, norm_gain, gate_weight, up_weight, down_weight, replica_plan, route_expert, replica_pick, combine_num):
    groups = lax.axis_size("dp")
    shards = lax.axis_size("ep")
    layers = norm_gain.shape[0]
    exp_host, units = gate_weight.shape[1:3]
    rep_host = replica_plan.shape[2]
    rows, width = tokens.shape
    count = groups * rows
    top = route_expert.shape[2]
    capacity = rows // 2
    sizes = (layers, groups, rows, top, exp_host, rep_host, capacity)

    numbers = combine_num.transpose(0, 2, 1).reshape(layers * top, rows).astype(bf16)
    numbers = jnp.pad(numbers, ((0, rows - layers * top), (0, lanes - rows)))
    payload = jnp.concatenate([tokens, numbers], axis=1)
    gathered = [payload]
    (ups,) = prefetch(0, payload, up_weight)
    for k in range(1, groups):
        gathered.append(xor_permute(payload, "dp", groups, k))
    gathered = jnp.concatenate(gathered, axis=0)
    stream = gathered[:, :width]
    number = gathered[:, width:]

    prepare = pl.pallas_call(
        functools.partial(setup_kernel, sizes=sizes),
        out_shape=(
            pltpu.VMEM((layers, exp_host, top, lanes), f32),
            pltpu.VMEM(norm_gain.shape, f32),
            pltpu.VMEM(gate_weight.shape[1:], bf16),
        ),
        in_specs=[any_spec()] + [hbm_spec()] * 5,
        out_specs=(vmem_spec(),) * 3,
        scratch_shapes=[
            pltpu.SMEM((layers, rep_host, groups), jnp.int32),
            pltpu.VMEM((layers, top, count), jnp.int32),
            pltpu.VMEM((layers, top, count), jnp.int32),
            pltpu.SemaphoreType.DMA((5,)),
        ],
        compiler_params=pltpu.CompilerParams(vmem_limit_bytes=4 * 2**20),
        cost_estimate=pl.CostEstimate(flops=4 * 10**9, bytes_accessed=2 * 10**7, transcendentals=0),
        name="setup",
    )
    small = (replica_plan, route_expert, replica_pick)
    small = [in_hbm(v.transpose(0, 2, 1)) for v in small] + [in_hbm(norm_gain), in_hbm(gate_weight)]
    mask, gains, gates = prepare(stream, *small)

    for layer in range(layers):
        xs = gather_shards(stream, shards)
        hidden = pl.pallas_call(
            functools.partial(
                gate_kernel, layer=layer, top=top, rows=rows, shards=shards, exp_host=exp_host, units=units, width=width
            ),
            out_shape=jax.ShapeDtypeStruct((exp_host * count, units), bf16),
            in_specs=[vmem_spec()] * (5 + shards),
            out_specs=vmem_spec(),
            scratch_shapes=[
                pltpu.VMEM((2, exp_host * units, lanes), f32),
            ],
            compiler_params=pltpu.CompilerParams(vmem_limit_bytes=8 * 2**20),
        )(mask, number, gains, *xs, gates, ups)
        (downs,) = prefetch(layer, hidden, down_weight)
        hs = gather_shards(hidden, shards)
        own, send = pl.pallas_call(
            functools.partial(
                down_kernel, layer=layer, shards=shards, exp_host=exp_host, units=units, width=width, tokens=count
            ),
            out_shape=(jax.ShapeDtypeStruct((count, width), f32), jax.ShapeDtypeStruct((count, width), bf16)),
            in_specs=[vmem_spec()] * (shards + 1),
            out_specs=(vmem_spec(), vmem_spec()),
            scratch_shapes=[
                pltpu.VMEM((width, lanes), f32),
            ],
            compiler_params=pltpu.CompilerParams(vmem_limit_bytes=8 * 2**20),
        )(*hs, downs)
        if layer + 1 < layers:
            gates, ups = prefetch(layer + 1, send, gate_weight, up_weight)
            update = own
            for k in range(1, groups):
                other = xor_permute(send, "dp", groups, k).astype(f32)
                blocks = [other[(b ^ k) * rows : ((b ^ k) + 1) * rows] for b in range(groups)]
                update = update + jnp.concatenate(blocks, axis=0)
        else:
            update = own[:rows]
            for k in range(1, groups):
                update = update + xor_permute(send[k * rows : (k + 1) * rows], "dp", groups, k).astype(f32)
            stream = stream[:rows]
        stream = (stream.astype(f32) + update).astype(bf16)
    return stream, update.astype(bf16)


def serve_table(plan_layer, groups, exp_host, rep_host):
    replicas = exp_host + rep_host
    flat = jnp.arange(groups * replicas, dtype=jnp.int32)
    host_of = flat // replicas
    local = flat % replicas
    copy = jnp.clip(local - exp_host, 0, rep_host - 1)
    copied = ((host_of - 1 - copy) % groups) * exp_host + plan_layer[host_of, copy]
    return jnp.where(local < exp_host, host_of * exp_host + local, copied)


def kept_slots(experts, picks, table, capacity):
    flat_e = experts.reshape(-1)
    matches = (table[None, :] == flat_e[:, None]).astype(jnp.int32)
    rank = jnp.cumsum(matches, axis=1) - 1
    wanted = picks.reshape(-1) % jnp.sum(matches, axis=1)
    chosen = matches * (rank == wanted[:, None]).astype(jnp.int32)
    before = jnp.cumsum(chosen, axis=0) - chosen
    return (jnp.sum(before * chosen, axis=1) < capacity).reshape(experts.shape)


def plain_device(tokens, norm_gain, gate_weight, up_weight, down_weight, replica_plan, route_expert, replica_pick, combine_num):
    groups = lax.axis_size("dp")
    host = lax.axis_index("dp")
    layers, _ = norm_gain.shape
    exp_host = gate_weight.shape[1]
    rep_host = replica_plan.shape[2]
    rows, _ = tokens.shape
    count = groups * rows
    top = route_expert.shape[2]
    stream = lax.all_gather(tokens, "dp", axis=0, tiled=True)
    numbers = lax.all_gather(combine_num, "dp", axis=1, tiled=True).astype(f32)
    own_ids = host * exp_host + jnp.arange(exp_host, dtype=jnp.int32)
    for layer in range(layers):
        table = serve_table(replica_plan[layer], groups, exp_host, rep_host)
        kept = jax.vmap(lambda e, p: kept_slots(e, p, table, rows // 2))(
            route_expert[layer].reshape(groups, rows, top), replica_pick[layer].reshape(groups, rows, top)
        ).reshape(count, top)
        weights = numbers[layer] / jnp.sum(numbers[layer], axis=1, keepdims=True) * kept
        hits = route_expert[layer][:, :, None] == own_ids[None, None, :]
        combine = jnp.sum(weights[:, :, None] * hits, axis=1)
        whole = lax.all_gather(stream, "ep", axis=1, tiled=True).astype(f32)
        inverse = lax.rsqrt(jnp.mean(whole * whole, axis=1, keepdims=True) + epsilon)
        normed = (whole * inverse * norm_gain[layer][None, :]).astype(bf16)
        gate = jnp.einsum("nd,rfd->rnf", normed, gate_weight[layer], preferred_element_type=f32)
        up = jnp.einsum("nd,rfd->rnf", normed, up_weight[layer], preferred_element_type=f32)
        hidden = (jax.nn.silu(gate) * up * combine.T[:, :, None]).astype(bf16)
        hidden = lax.all_gather(hidden, "ep", axis=2, tiled=True)
        partial = jnp.einsum("rnf,rdf->nd", hidden, down_weight[layer], preferred_element_type=f32)
        parts = lax.all_gather(partial.astype(bf16), "dp", axis=0).astype(f32)
        update = jnp.sum(parts, axis=0)
        stream = (stream.astype(f32) + update).astype(bf16)
    stream = lax.dynamic_slice_in_dim(stream, host * rows, rows, 0)
    update = lax.dynamic_slice_in_dim(update, host * rows, rows, 0)
    return stream, update.astype(bf16)


def per_device(*args):
    tokens, norm_gain, gate_weight = args[:3]
    groups, shards = lax.axis_size("dp"), lax.axis_size("ep")
    layers, units = norm_gain.shape[0], gate_weight.shape[2]
    rows, width = tokens.shape
    fits = (
        groups & (groups - 1) == 0
        and shards & (shards - 1) == 0
        and 2 <= shards <= widest
        and width % lanes == 0
        and units % lanes == 0
        and rows % 16 == 0
        and groups * rows <= lanes
        and layers * args[6].shape[2] <= rows
        and args[6].shape[2] % 8 == 0
    )
    return fast_device(*args) if fits else plain_device(*args)


def solution(mesh):
    return jax.shard_map(
        per_device,
        mesh=mesh,
        in_specs=(
            P("dp", "ep"),
            P(),
            P(None, "dp", "ep", None),
            P(None, "dp", "ep", None),
            P(None, "dp", "ep", None),
            P(),
            P(),
            P(),
            P(None, "dp", None),
        ),
        out_specs=(P("dp", "ep"), P("dp", "ep")),
        check_vma=False,
    )
```

profile of v0, /device:TPU:0, one launch (start us, length us, event | category | flops | bytes accessed | tf_op | source)
XLA Modules:
  0.0 106.9 jit_solution(17403283101754448946)
XLA Ops:
  0.6 0.7 convert_bitcast_fusion
  1.3 0.8 pad_maximum_fusion.1.refs_0_
  2.1 5.1 %collective-permute-start.2 = (bf16[16,1024]{1,0:T(8,128)(2,1)S(1)}, bf16[16,1024]{1,0:T(8,128)(2,1)S(1)}, u32[]{:S(2)}, u32[]{:S(2)}) collective-permute-start(bf16[16,1024]{1,0:T(8,128)(2,1)S(1)} %pad_maximum_fusion.1.refs_0_), channel_id=1, source_target_pairs={{0,3},{1,2},{2,1},{3,0},{4,7},{5,6},{6,5},{7,4},{8,11},{9,10},{10,... | collective-permute-start | bytes 98312 | tf_op jit(solution)/shard_map/ppermute | solution.py:198
  7.2 0.6 collective-permute-start
  7.7 1.3 %collective-permute-done.2 = bf16[16,1024]{1,0:T(8,128)(2,1)S(1)} collective-permute-done((bf16[16,1024]{1,0:T(8,128)(2,1)S(1)}, bf16[16,1024]{1,0:T(8,128)(2,1)S(1)}, u32[]{:S(2)}, u32[]{:S(2)}) %collective-permute-start.2) | collective-permute-done | bytes 32800 | tf_op jit(solution)/shard_map/ppermute | solution.py:198
  9.1 2.9 %collective-permute-done.1 = bf16[16,1024]{1,0:T(8,128)(2,1)S(1)} collective-permute-done((bf16[16,1024]{1,0:T(8,128)(2,1)S(1)}, bf16[16,1024]{1,0:T(8,128)(2,1)S(1)}, u32[]{:S(2)}, u32[]{:S(2)}) %collective-permute-start.1) | collective-permute-done | bytes 32800 | tf_op jit(solution)/shard_map/ppermute | solution.py:198
  12.0 0.8 pad_maximum_fusion
  12.8 2.5 %collective-permute-start.8 = (bf16[64,896]{1,0:T(8,128)(2,1)S(1)}, bf16[64,896]{1,0:T(8,128)(2,1)S(1)}, u32[]{:S(2)}, u32[]{:S(2)}) collective-permute-start(bf16[64,896]{1,0:T(8,128)(2,1)S(1)} %slice.72._.refs_0_), channel_id=1, source_target_pairs={{0,24},{4,28},{8,16},{12,20},{16,8},{20,12},{24,0},{28,4},{1,25},{... | collective-permute-start | bytes 344072 | tf_op jit(solution)/shard_map/ppermute | solution.py:198
  15.3 0.5 collective-permute-start.6
  15.8 0.5 collective-permute-start.4
  16.3 4.1 %shard_map.104.refs_9_ = bf16[3,256,7168]{2,1,0:T(8,128)(2,1)S(1)} custom-call(bf16[16,1024]{1,0:T(8,128)(2,1)S(1)} %pad_maximum_fusion.1.refs_0_, bf16[2,3,256,7168]{3,2,1,0:T(8,128)(2,1)} %refs_2_.1), custom_call_target="tpu_custom_call" | custom-call | flops 4404019200 | bytes 22020096 | tf_op jit(solution)/shard_map/pallas_call | solution.py:186
  20.6 0.5 collective-permute-start.9
  21.1 0.4 collective-permute-start.5
  21.6 4.2 %setup.1 = (f32[2,3,8,128]{3,2,1,0:T(8,128)S(1)}, f32[2,7168]{1,0:T(2,128)S(1)}, bf16[3,256,7168]{2,1,0:T(8,128)(2,1)S(1)}) custom-call(bf16[64,896]{1,0:T(8,128)(2,1)S(1)} %slice.72._.refs_0_, s32[2,2,4]{2,1,0:T(2,128)} %bitcast.9, s32[2,8,64]{2,1,0:T(8,128)} %bitcast.7, s32[2,8,64]{2,1,0:T(8,128)} %bitcast.8, f32[2,7168]{1,0:T(2,128)} %gain_hbm.1, ...), custom_call_target="tpu_custom_call" | custom-call | flops 4000000000 | bytes 20000000 | tf_op jit(solution)/shard_map/setup/pallas_call | solution.py:256
  25.9 6.1 %shard_map.105.refs_0_ = bf16[192,256]{1,0:T(8,128)(2,1)S(1)} custom-call(f32[2,3,8,128]{3,2,1,0:T(8,128)S(1)} %get-tuple-element.11.mask_ref, bf16[64,128]{1,0:T(8,128)(2,1)S(1)} %pad_maximum_fusion.2.num_ref, f32[2,7168]{1,0:T(2,128)S(1)} %get-tuple-element.12.gain_ref, bf16[64,896]{1,0:T(8,128)(2,1)S(1)} %slice.72._.refs_0_, ...), custom_call_target="tpu_custom_call" | custom-call | tf_op jit(solution)/shard_map/pallas_call | solution.py:260
  32.0 2.5 %collective-permute-start.15 = (bf16[192,256]{1,0:T(8,128)(2,1)S(1)}, bf16[192,256]{1,0:T(8,128)(2,1)S(1)}, u32[]{:S(2)}, u32[]{:S(2)}) collective-permute-start(bf16[192,256]{1,0:T(8,128)(2,1)S(1)} %shard_map.105.refs_0_), channel_id=1, source_target_pairs={{0,24},{4,28},{8,16},{12,20},{16,8},{20,12},{24,0},{28,4},{1,25},{... | collective-permute-start | bytes 294920 | tf_op jit(solution)/shard_map/ppermute | solution.py:198
  34.5 0.5 collective-permute-start.13
  35.0 0.6 collective-permute-start.11
  35.6 2.3 %collective-permute-done.15.refs_6_ = bf16[192,256]{1,0:T(8,128)(2,1)S(1)} collective-permute-done((bf16[192,256]{1,0:T(8,128)(2,1)S(1)}, bf16[192,256]{1,0:T(8,128)(2,1)S(1)}, u32[]{:S(2)}, u32[]{:S(2)}) %collective-permute-start.15) | collective-permute-done | bytes 98336 | tf_op jit(solution)/shard_map/ppermute | solution.py:198
  37.9 2.0 %collective-permute-done.13.refs_4_ = bf16[192,256]{1,0:T(8,128)(2,1)S(1)} collective-permute-done((bf16[192,256]{1,0:T(8,128)(2,1)S(1)}, bf16[192,256]{1,0:T(8,128)(2,1)S(1)}, u32[]{:S(2)}, u32[]{:S(2)}) %collective-permute-start.13) | collective-permute-done | bytes 98336 | tf_op jit(solution)/shard_map/ppermute | solution.py:198
  39.9 0.5 collective-permute-start.12
  40.4 4.1 %shard_map.106.refs_8_ = bf16[3,896,2048]{2,1,0:T(8,128)(2,1)S(1)} custom-call(bf16[192,256]{1,0:T(8,128)(2,1)S(1)} %shard_map.105.refs_0_, bf16[2,3,896,2048]{3,2,1,0:T(8,128)(2,1)} %refs_1_.7), custom_call_target="tpu_custom_call" | custom-call | flops 4404019200 | bytes 22020096 | tf_op jit(solution)/shard_map/pallas_call | solution.py:186
  44.6 3.3 %shard_map.107 = (f32[64,896]{1,0:T(8,128)S(1)}, bf16[64,896]{1,0:T(8,128)(2,1)S(1)}) custom-call(bf16[192,256]{1,0:T(8,128)(2,1)S(1)} %shard_map.105.refs_0_, bf16[192,256]{1,0:T(8,128)(2,1)S(1)} %collective-permute-done.10.refs_1_, bf16[192,256]{1,0:T(8,128)(2,1)S(1)} %collective-permute-done.11.refs_2_, ...), custom_call_target="tpu_custom_call" | custom-call | tf_op jit(solution)/shard_map/pallas_call | solution.py:274
  47.9 2.1 %collective-permute-start.18 = (bf16[64,896]{1,0:T(8,128)(2,1)S(1)}, bf16[64,896]{1,0:T(8,128)(2,1)S(1)}, u32[]{:S(2)}, u32[]{:S(2)}) collective-permute-start(bf16[64,896]{1,0:T(8,128)(2,1)S(1)} %get-tuple-element.15.refs_0_), channel_id=1, source_target_pairs={{0,2},{1,3},{2,0},{3,1},{4,6},{5,7},{6,4},{7,5},{8,10},{9,11},{10,... | collective-permute-start | bytes 344072 | tf_op jit(solution)/shard_map/ppermute | solution.py:198
  50.1 1.3 %collective-permute-start.17 = (bf16[64,896]{1,0:T(8,128)(2,1)S(1)}, bf16[64,896]{1,0:T(8,128)(2,1)S(1)}, u32[]{:S(2)}, u32[]{:S(2)}) collective-permute-start(bf16[64,896]{1,0:T(8,128)(2,1)S(1)} %get-tuple-element.15.refs_0_), channel_id=1, source_target_pairs={{0,1},{1,0},{2,3},{3,2},{4,5},{5,4},{6,7},{7,6},{8,9},{9,8},{10,11... | collective-permute-start | bytes 344072 | tf_op jit(solution)/shard_map/ppermute | solution.py:198
  51.4 6.9 %collective-permute-done.18 = bf16[64,896]{1,0:T(8,128)(2,1)S(1)} collective-permute-done((bf16[64,896]{1,0:T(8,128)(2,1)S(1)}, bf16[64,896]{1,0:T(8,128)(2,1)S(1)}, u32[]{:S(2)}, u32[]{:S(2)}) %collective-permute-start.18) | collective-permute-done | bytes 114720 | tf_op jit(solution)/shard_map/ppermute | solution.py:198
  58.4 1.2 %collective-permute-done.17 = bf16[64,896]{1,0:T(8,128)(2,1)S(1)} collective-permute-done((bf16[64,896]{1,0:T(8,128)(2,1)S(1)}, bf16[64,896]{1,0:T(8,128)(2,1)S(1)}, u32[]{:S(2)}, u32[]{:S(2)}) %collective-permute-start.17) | collective-permute-done | bytes 114720 | tf_op jit(solution)/shard_map/ppermute | solution.py:198
  59.7 1.8 %collective-permute-start.25 = (bf16[64,896]{1,0:T(8,128)(2,1)S(1)}, bf16[64,896]{1,0:T(8,128)(2,1)S(1)}, u32[]{:S(2)}, u32[]{:S(2)}) collective-permute-start(bf16[64,896]{1,0:T(8,128)(2,1)S(1)} %fusion.3.refs_0_), channel_id=1, source_target_pairs={{0,24},{4,28},{8,16},{12,20},{16,8},{20,12},{24,0},{28,4},{1,25},{... | collective-permute-start | bytes 344072 | tf_op jit(solution)/shard_map/ppermute | solution.py:198
  61.5 1.3 %collective-permute-start.23 = (bf16[64,896]{1,0:T(8,128)(2,1)S(1)}, bf16[64,896]{1,0:T(8,128)(2,1)S(1)}, u32[]{:S(2)}, u32[]{:S(2)}) collective-permute-start(bf16[64,896]{1,0:T(8,128)(2,1)S(1)} %fusion.3.refs_0_), channel_id=1, source_target_pairs={{0,16},{4,20},{8,24},{12,28},{16,0},{20,4},{24,8},{28,12},{1,17},{... | collective-permute-start | bytes 344072 | tf_op jit(solution)/shard_map/ppermute | solution.py:198
  62.8 0.5 collective-permute-start.21
  63.3 3.3 %collective-permute-done.25.refs_6_ = bf16[64,896]{1,0:T(8,128)(2,1)S(1)} collective-permute-done((bf16[64,896]{1,0:T(8,128)(2,1)S(1)}, bf16[64,896]{1,0:T(8,128)(2,1)S(1)}, u32[]{:S(2)}, u32[]{:S(2)}) %collective-permute-start.25) | collective-permute-done | bytes 114720 | tf_op jit(solution)/shard_map/ppermute | solution.py:198
  66.6 0.6 collective-permute-done.23.refs_4_
  67.2 0.4 collective-permute-done.21.refs_2_
  67.7 7.3 %shard_map.108 = (bf16[3,256,7168]{2,1,0:T(8,128)(2,1)S(1)}, bf16[3,256,7168]{2,1,0:T(8,128)(2,1)S(1)}) custom-call(bf16[64,896]{1,0:T(8,128)(2,1)S(1)} %get-tuple-element.15.refs_0_, bf16[2,3,256,7168]{3,2,1,0:T(8,128)(2,1)} %refs_1_.6, bf16[2,3,256,7168]{3,2,1,0:T(8,128)(2,1)} %refs_2_.1), custom_call_target="tpu_custom_call" | custom-call | flops 8808038400 | bytes 44040192 | tf_op jit(solution)/shard_map/pallas_call | solution.py:186
  75.0 6.4 %shard_map.109.refs_0_ = bf16[192,256]{1,0:T(8,128)(2,1)S(1)} custom-call(f32[2,3,8,128]{3,2,1,0:T(8,128)S(1)} %get-tuple-element.11.mask_ref, bf16[64,128]{1,0:T(8,128)(2,1)S(1)} %pad_maximum_fusion.2.num_ref, f32[2,7168]{1,0:T(2,128)S(1)} %get-tuple-element.12.gain_ref, bf16[64,896]{1,0:T(8,128)(2,1)S(1)} %fusion.3.refs_0_, ...), custom_call_target="tpu_custom_call" | custom-call | tf_op jit(solution)/shard_map/pallas_call | solution.py:260
  81.4 1.8 %collective-permute-start.32 = (bf16[192,256]{1,0:T(8,128)(2,1)S(1)}, bf16[192,256]{1,0:T(8,128)(2,1)S(1)}, u32[]{:S(2)}, u32[]{:S(2)}) collective-permute-start(bf16[192,256]{1,0:T(8,128)(2,1)S(1)} %shard_map.109.refs_0_), channel_id=1, source_target_pairs={{0,24},{4,28},{8,16},{12,20},{16,8},{20,12},{24,0},{28,4},{1,25},{... | collective-permute-start | bytes 294920 | tf_op jit(solution)/shard_map/ppermute | solution.py:198
  83.1 1.3 %collective-permute-start.30 = (bf16[192,256]{1,0:T(8,128)(2,1)S(1)}, bf16[192,256]{1,0:T(8,128)(2,1)S(1)}, u32[]{:S(2)}, u32[]{:S(2)}) collective-permute-start(bf16[192,256]{1,0:T(8,128)(2,1)S(1)} %shard_map.109.refs_0_), channel_id=1, source_target_pairs={{0,16},{4,20},{8,24},{12,28},{16,0},{20,4},{24,8},{28,12},{1,17},{... | collective-permute-start | bytes 294920 | tf_op jit(solution)/shard_map/ppermute | solution.py:198
  84.4 0.5 collective-permute-start.28
  84.9 3.1 %collective-permute-done.32.refs_6_ = bf16[192,256]{1,0:T(8,128)(2,1)S(1)} collective-permute-done((bf16[192,256]{1,0:T(8,128)(2,1)S(1)}, bf16[192,256]{1,0:T(8,128)(2,1)S(1)}, u32[]{:S(2)}, u32[]{:S(2)}) %collective-permute-start.32) | collective-permute-done | bytes 98336 | tf_op jit(solution)/shard_map/ppermute | solution.py:198
  88.0 1.5 %collective-permute-done.30.refs_4_ = bf16[192,256]{1,0:T(8,128)(2,1)S(1)} collective-permute-done((bf16[192,256]{1,0:T(8,128)(2,1)S(1)}, bf16[192,256]{1,0:T(8,128)(2,1)S(1)}, u32[]{:S(2)}, u32[]{:S(2)}) %collective-permute-start.30) | collective-permute-done | bytes 98336 | tf_op jit(solution)/shard_map/ppermute | solution.py:198
  89.5 0.5 collective-permute-start.29
  90.0 4.1 %shard_map.110.refs_8_ = bf16[3,896,2048]{2,1,0:T(8,128)(2,1)S(1)} custom-call(bf16[192,256]{1,0:T(8,128)(2,1)S(1)} %shard_map.109.refs_0_, bf16[2,3,896,2048]{3,2,1,0:T(8,128)(2,1)} %refs_1_.7), custom_call_target="tpu_custom_call" | custom-call | flops 4404019200 | bytes 22020096 | tf_op jit(solution)/shard_map/pallas_call | solution.py:186
  94.2 3.3 %shard_map.111 = (f32[64,896]{1,0:T(8,128)S(1)}, bf16[64,896]{1,0:T(8,128)(2,1)S(1)}) custom-call(bf16[192,256]{1,0:T(8,128)(2,1)S(1)} %shard_map.109.refs_0_, bf16[192,256]{1,0:T(8,128)(2,1)S(1)} %collective-permute-done.27.refs_1_, bf16[192,256]{1,0:T(8,128)(2,1)S(1)} %collective-permute-done.28.refs_2_, ...), custom_call_target="tpu_custom_call" | custom-call | tf_op jit(solution)/shard_map/pallas_call | solution.py:274
  97.5 2.4 %collective-permute-start.34 = (bf16[16,896]{1,0:T(8,128)(2,1)S(1)}, bf16[16,896]{1,0:T(8,128)(2,1)S(1)}, u32[]{:S(2)}, u32[]{:S(2)}) collective-permute-start(bf16[16,896]{1,0:T(8,128)(2,1)S(1)} %get-tuple-element.22), channel_id=1, source_target_pairs={{0,1},{1,0},{2,3},{3,2},{4,5},{5,4},{6,7},{7,6},{8,9},{9,8},{10,11... | collective-permute-start | bytes 86024 | tf_op jit(solution)/shard_map/ppermute | solution.py:198
  99.9 1.6 %collective-permute-start.36 = (bf16[16,896]{1,0:T(8,128)(2,1)S(1)}, bf16[16,896]{1,0:T(8,128)(2,1)S(1)}, u32[]{:S(2)}, u32[]{:S(2)}) collective-permute-start(bf16[16,896]{1,0:T(8,128)(2,1)S(1)} %get-tuple-element.23), channel_id=1, source_target_pairs={{0,3},{1,2},{2,1},{3,0},{4,7},{5,6},{6,5},{7,4},{8,11},{9,10},{10,... | collective-permute-start | bytes 86024 | tf_op jit(solution)/shard_map/ppermute | solution.py:198
  101.8 3.8 %collective-permute-done.36 = bf16[16,896]{1,0:T(8,128)(2,1)S(1)} collective-permute-done((bf16[16,896]{1,0:T(8,128)(2,1)S(1)}, bf16[16,896]{1,0:T(8,128)(2,1)S(1)}, u32[]{:S(2)}, u32[]{:S(2)}) %collective-permute-start.36) | collective-permute-done | bytes 28704 | tf_op jit(solution)/shard_map/ppermute | solution.py:198
  105.6 0.7 collective-permute-done.35
  106.3 0.6 fusion.4
  (49 shorter events, 1.0 us)
Async XLA Ops:
  2.1 7.0 %collective-permute-start.2 = (bf16[16,1024]{1,0:T(8,128)(2,1)S(1)}, bf16[16,1024]{1,0:T(8,128)(2,1)S(1)}, u32[]{:S(2)}, u32[]{:S(2)}) collective-permute-start(bf16[16,1024]{1,0:T(8,128)(2,1)S(1)} %pad_maximum_fusion.1.refs_0_), channel_id=1, source_target_pairs={{0,3},{1,2},{2,1},{3,0},{4,7},{5,6},{6,5},{7,4},{8,11},{9,10},{10,... | collective-permute-start | bytes 98312 | tf_op jit(solution)/shard_map/ppermute | solution.py:198
  7.2 4.8 %collective-permute-start.1 = (bf16[16,1024]{1,0:T(8,128)(2,1)S(1)}, bf16[16,1024]{1,0:T(8,128)(2,1)S(1)}, u32[]{:S(2)}, u32[]{:S(2)}) collective-permute-start(bf16[16,1024]{1,0:T(8,128)(2,1)S(1)} %pad_maximum_fusion.1.refs_0_), channel_id=1, source_target_pairs={{0,2},{1,3},{2,0},{3,1},{4,6},{5,7},{6,4},{7,5},{8,10},{9,11},{10,... | collective-permute-start | bytes 98312 | tf_op jit(solution)/shard_map/ppermute | solution.py:198
  7.2 4.8 %collective-permute-start = (bf16[16,1024]{1,0:T(8,128)(2,1)S(1)}, bf16[16,1024]{1,0:T(8,128)(2,1)S(1)}, u32[]{:S(2)}, u32[]{:S(2)}) collective-permute-start(bf16[16,1024]{1,0:T(8,128)(2,1)S(1)} %pad_maximum_fusion.1.refs_0_), channel_id=1, source_target_pairs={{0,1},{1,0},{2,3},{3,2},{4,5},{5,4},{6,7},{7,6},{8,9},{9,8},{10,11... | collective-permute-start | bytes 98312 | tf_op jit(solution)/shard_map/ppermute | solution.py:198
  12.8 7.8 %collective-permute-start.8 = (bf16[64,896]{1,0:T(8,128)(2,1)S(1)}, bf16[64,896]{1,0:T(8,128)(2,1)S(1)}, u32[]{:S(2)}, u32[]{:S(2)}) collective-permute-start(bf16[64,896]{1,0:T(8,128)(2,1)S(1)} %slice.72._.refs_0_), channel_id=1, source_target_pairs={{0,24},{4,28},{8,16},{12,20},{16,8},{20,12},{24,0},{28,4},{1,25},{... | collective-permute-start | bytes 344072 | tf_op jit(solution)/shard_map/ppermute | solution.py:198
  15.3 5.8 %collective-permute-start.6 = (bf16[64,896]{1,0:T(8,128)(2,1)S(1)}, bf16[64,896]{1,0:T(8,128)(2,1)S(1)}, u32[]{:S(2)}, u32[]{:S(2)}) collective-permute-start(bf16[64,896]{1,0:T(8,128)(2,1)S(1)} %slice.72._.refs_0_), channel_id=1, source_target_pairs={{0,16},{4,20},{8,24},{12,28},{16,0},{20,4},{24,8},{28,12},{1,17},{... | collective-permute-start | bytes 344072 | tf_op jit(solution)/shard_map/ppermute | solution.py:198
  15.8 5.4 %collective-permute-start.4 = (bf16[64,896]{1,0:T(8,128)(2,1)S(1)}, bf16[64,896]{1,0:T(8,128)(2,1)S(1)}, u32[]{:S(2)}, u32[]{:S(2)}) collective-permute-start(bf16[64,896]{1,0:T(8,128)(2,1)S(1)} %slice.72._.refs_0_), channel_id=1, source_target_pairs={{0,8},{4,12},{8,0},{12,4},{16,24},{20,28},{24,16},{28,20},{1,9},{5... | collective-permute-start | bytes 344072 | tf_op jit(solution)/shard_map/ppermute | solution.py:198
  20.5 5.4 %collective-permute-start.3 = (bf16[64,896]{1,0:T(8,128)(2,1)S(1)}, bf16[64,896]{1,0:T(8,128)(2,1)S(1)}, u32[]{:S(2)}, u32[]{:S(2)}) collective-permute-start(bf16[64,896]{1,0:T(8,128)(2,1)S(1)} %slice.72._.refs_0_), channel_id=1, source_target_pairs={{0,4},{4,0},{8,12},{12,8},{16,20},{20,16},{24,28},{28,24},{1,5},{5... | collective-permute-start | bytes 344072 | tf_op jit(solution)/shard_map/ppermute | solution.py:198
  20.6 5.3 %collective-permute-start.9 = (bf16[64,896]{1,0:T(8,128)(2,1)S(1)}, bf16[64,896]{1,0:T(8,128)(2,1)S(1)}, u32[]{:S(2)}, u32[]{:S(2)}) collective-permute-start(bf16[64,896]{1,0:T(8,128)(2,1)S(1)} %collective-permute-done.8.refs_6_), channel_id=1, source_target_pairs={{0,4},{4,0},{8,12},{12,8},{16,20},{20,16},{24,28},{28,24},{1,5},{5... | collective-permute-start | bytes 344072 | tf_op jit(solution)/shard_map/ppermute | solution.py:198
  21.0 4.8 %collective-permute-start.7 = (bf16[64,896]{1,0:T(8,128)(2,1)S(1)}, bf16[64,896]{1,0:T(8,128)(2,1)S(1)}, u32[]{:S(2)}, u32[]{:S(2)}) collective-permute-start(bf16[64,896]{1,0:T(8,128)(2,1)S(1)} %collective-permute-done.6.refs_4_), channel_id=1, source_target_pairs={{0,4},{4,0},{8,12},{12,8},{16,20},{20,16},{24,28},{28,24},{1,5},{5... | collective-permute-start | bytes 344072 | tf_op jit(solution)/shard_map/ppermute | solution.py:198
  21.1 4.7 %collective-permute-start.5 = (bf16[64,896]{1,0:T(8,128)(2,1)S(1)}, bf16[64,896]{1,0:T(8,128)(2,1)S(1)}, u32[]{:S(2)}, u32[]{:S(2)}) collective-permute-start(bf16[64,896]{1,0:T(8,128)(2,1)S(1)} %collective-permute-done.4.refs_2_), channel_id=1, source_target_pairs={{0,4},{4,0},{8,12},{12,8},{16,20},{20,16},{24,28},{28,24},{1,5},{5... | collective-permute-start | bytes 344072 | tf_op jit(solution)/shard_map/ppermute | solution.py:198
  21.6 4.3 %copy-start = (bf16[16,896]{1,0:T(8,128)(2,1)S(1)}, bf16[16,896]{1,0:T(8,128)(2,1)}, u32[]{:S(2)}) copy-start(bf16[16,896]{1,0:T(8,128)(2,1)} %param.9) | copy-start | bytes 86020
  32.0 5.8 %collective-permute-start.15 = (bf16[192,256]{1,0:T(8,128)(2,1)S(1)}, bf16[192,256]{1,0:T(8,128)(2,1)S(1)}, u32[]{:S(2)}, u32[]{:S(2)}) collective-permute-start(bf16[192,256]{1,0:T(8,128)(2,1)S(1)} %shard_map.105.refs_0_), channel_id=1, source_target_pairs={{0,24},{4,28},{8,16},{12,20},{16,8},{20,12},{24,0},{28,4},{1,25},{... | collective-permute-start | bytes 294920 | tf_op jit(solution)/shard_map/ppermute | solution.py:198
  34.5 5.4 %collective-permute-start.13 = (bf16[192,256]{1,0:T(8,128)(2,1)S(1)}, bf16[192,256]{1,0:T(8,128)(2,1)S(1)}, u32[]{:S(2)}, u32[]{:S(2)}) collective-permute-start(bf16[192,256]{1,0:T(8,128)(2,1)S(1)} %shard_map.105.refs_0_), channel_id=1, source_target_pairs={{0,16},{4,20},{8,24},{12,28},{16,0},{20,4},{24,8},{28,12},{1,17},{... | collective-permute-start | bytes 294920 | tf_op jit(solution)/shard_map/ppermute | solution.py:198
  35.0 4.9 %collective-permute-start.11 = (bf16[192,256]{1,0:T(8,128)(2,1)S(1)}, bf16[192,256]{1,0:T(8,128)(2,1)S(1)}, u32[]{:S(2)}, u32[]{:S(2)}) collective-permute-start(bf16[192,256]{1,0:T(8,128)(2,1)S(1)} %shard_map.105.refs_0_), channel_id=1, source_target_pairs={{0,8},{4,12},{8,0},{12,4},{16,24},{20,28},{24,16},{28,20},{1,9},{5... | collective-permute-start | bytes 294920 | tf_op jit(solution)/shard_map/ppermute | solution.py:198
  35.6 9.0 %collective-permute-start.10 = (bf16[192,256]{1,0:T(8,128)(2,1)S(1)}, bf16[192,256]{1,0:T(8,128)(2,1)S(1)}, u32[]{:S(2)}, u32[]{:S(2)}) collective-permute-start(bf16[192,256]{1,0:T(8,128)(2,1)S(1)} %shard_map.105.refs_0_), channel_id=1, source_target_pairs={{0,4},{4,0},{8,12},{12,8},{16,20},{20,16},{24,28},{28,24},{1,5},{5... | collective-permute-start | bytes 294920 | tf_op jit(solution)/shard_map/ppermute | solution.py:198
  37.9 6.7 %collective-permute-start.16 = (bf16[192,256]{1,0:T(8,128)(2,1)S(1)}, bf16[192,256]{1,0:T(8,128)(2,1)S(1)}, u32[]{:S(2)}, u32[]{:S(2)}) collective-permute-start(bf16[192,256]{1,0:T(8,128)(2,1)S(1)} %collective-permute-done.15.refs_6_), channel_id=1, source_target_pairs={{0,4},{4,0},{8,12},{12,8},{16,20},{20,16},{24,28},{28,24},{1,5},{5... | collective-permute-start | bytes 294920 | tf_op jit(solution)/shard_map/ppermute | solution.py:198
  39.9 4.7 %collective-permute-start.14 = (bf16[192,256]{1,0:T(8,128)(2,1)S(1)}, bf16[192,256]{1,0:T(8,128)(2,1)S(1)}, u32[]{:S(2)}, u32[]{:S(2)}) collective-permute-start(bf16[192,256]{1,0:T(8,128)(2,1)S(1)} %collective-permute-done.13.refs_4_), channel_id=1, source_target_pairs={{0,4},{4,0},{8,12},{12,8},{16,20},{20,16},{24,28},{28,24},{1,5},{5... | collective-permute-start | bytes 294920 | tf_op jit(solution)/shard_map/ppermute | solution.py:198
  39.9 4.7 %collective-permute-start.12 = (bf16[192,256]{1,0:T(8,128)(2,1)S(1)}, bf16[192,256]{1,0:T(8,128)(2,1)S(1)}, u32[]{:S(2)}, u32[]{:S(2)}) collective-permute-start(bf16[192,256]{1,0:T(8,128)(2,1)S(1)} %collective-permute-done.11.refs_2_), channel_id=1, source_target_pairs={{0,4},{4,0},{8,12},{12,8},{16,20},{20,16},{24,28},{28,24},{1,5},{5... | collective-permute-start | bytes 294920 | tf_op jit(solution)/shard_map/ppermute | solution.py:198
  47.9 10.4 %collective-permute-start.18 = (bf16[64,896]{1,0:T(8,128)(2,1)S(1)}, bf16[64,896]{1,0:T(8,128)(2,1)S(1)}, u32[]{:S(2)}, u32[]{:S(2)}) collective-permute-start(bf16[64,896]{1,0:T(8,128)(2,1)S(1)} %get-tuple-element.15.refs_0_), channel_id=1, source_target_pairs={{0,2},{1,3},{2,0},{3,1},{4,6},{5,7},{6,4},{7,5},{8,10},{9,11},{10,... | collective-permute-start | bytes 344072 | tf_op jit(solution)/shard_map/ppermute | solution.py:198
  50.0 8.4 %collective-permute-start.19 = (bf16[64,896]{1,0:T(8,128)(2,1)S(1)}, bf16[64,896]{1,0:T(8,128)(2,1)S(1)}, u32[]{:S(2)}, u32[]{:S(2)}) collective-permute-start(bf16[64,896]{1,0:T(8,128)(2,1)S(1)} %get-tuple-element.15.refs_0_), channel_id=1, source_target_pairs={{0,3},{1,2},{2,1},{3,0},{4,7},{5,6},{6,5},{7,4},{8,11},{9,10},{10,... | collective-permute-start | bytes 344072 | tf_op jit(solution)/shard_map/ppermute | solution.py:198
  50.1 9.5 %collective-permute-start.17 = (bf16[64,896]{1,0:T(8,128)(2,1)S(1)}, bf16[64,896]{1,0:T(8,128)(2,1)S(1)}, u32[]{:S(2)}, u32[]{:S(2)}) collective-permute-start(bf16[64,896]{1,0:T(8,128)(2,1)S(1)} %get-tuple-element.15.refs_0_), channel_id=1, source_target_pairs={{0,1},{1,0},{2,3},{3,2},{4,5},{5,4},{6,7},{7,6},{8,9},{9,8},{10,11... | collective-permute-start | bytes 344072 | tf_op jit(solution)/shard_map/ppermute | solution.py:198
  59.7 6.9 %collective-permute-start.25 = (bf16[64,896]{1,0:T(8,128)(2,1)S(1)}, bf16[64,896]{1,0:T(8,128)(2,1)S(1)}, u32[]{:S(2)}, u32[]{:S(2)}) collective-permute-start(bf16[64,896]{1,0:T(8,128)(2,1)S(1)} %fusion.3.refs_0_), channel_id=1, source_target_pairs={{0,24},{4,28},{8,16},{12,20},{16,8},{20,12},{24,0},{28,4},{1,25},{... | collective-permute-start | bytes 344072 | tf_op jit(solution)/shard_map/ppermute | solution.py:198
  61.5 5.7 %collective-permute-start.23 = (bf16[64,896]{1,0:T(8,128)(2,1)S(1)}, bf16[64,896]{1,0:T(8,128)(2,1)S(1)}, u32[]{:S(2)}, u32[]{:S(2)}) collective-permute-start(bf16[64,896]{1,0:T(8,128)(2,1)S(1)} %fusion.3.refs_0_), channel_id=1, source_target_pairs={{0,16},{4,20},{8,24},{12,28},{16,0},{20,4},{24,8},{28,12},{1,17},{... | collective-permute-start | bytes 344072 | tf_op jit(solution)/shard_map/ppermute | solution.py:198
  62.8 4.8 %collective-permute-start.21 = (bf16[64,896]{1,0:T(8,128)(2,1)S(1)}, bf16[64,896]{1,0:T(8,128)(2,1)S(1)}, u32[]{:S(2)}, u32[]{:S(2)}) collective-permute-start(bf16[64,896]{1,0:T(8,128)(2,1)S(1)} %fusion.3.refs_0_), channel_id=1, source_target_pairs={{0,8},{4,12},{8,0},{12,4},{16,24},{20,28},{24,16},{28,20},{1,9},{5... | collective-permute-start | bytes 344072 | tf_op jit(solution)/shard_map/ppermute | solution.py:198
  63.3 11.7 %collective-permute-start.20 = (bf16[64,896]{1,0:T(8,128)(2,1)S(1)}, bf16[64,896]{1,0:T(8,128)(2,1)S(1)}, u32[]{:S(2)}, u32[]{:S(2)}) collective-permute-start(bf16[64,896]{1,0:T(8,128)(2,1)S(1)} %fusion.3.refs_0_), channel_id=1, source_target_pairs={{0,4},{4,0},{8,12},{12,8},{16,20},{20,16},{24,28},{28,24},{1,5},{5... | collective-permute-start | bytes 344072 | tf_op jit(solution)/shard_map/ppermute | solution.py:198
  66.6 8.4 %collective-permute-start.26 = (bf16[64,896]{1,0:T(8,128)(2,1)S(1)}, bf16[64,896]{1,0:T(8,128)(2,1)S(1)}, u32[]{:S(2)}, u32[]{:S(2)}) collective-permute-start(bf16[64,896]{1,0:T(8,128)(2,1)S(1)} %collective-permute-done.25.refs_6_), channel_id=1, source_target_pairs={{0,4},{4,0},{8,12},{12,8},{16,20},{20,16},{24,28},{28,24},{1,5},{5... | collective-permute-start | bytes 344072 | tf_op jit(solution)/shard_map/ppermute | solution.py:198
  67.2 7.8 %collective-permute-start.24 = (bf16[64,896]{1,0:T(8,128)(2,1)S(1)}, bf16[64,896]{1,0:T(8,128)(2,1)S(1)}, u32[]{:S(2)}, u32[]{:S(2)}) collective-permute-start(bf16[64,896]{1,0:T(8,128)(2,1)S(1)} %collective-permute-done.23.refs_4_), channel_id=1, source_target_pairs={{0,4},{4,0},{8,12},{12,8},{16,20},{20,16},{24,28},{28,24},{1,5},{5... | collective-permute-start | bytes 344072 | tf_op jit(solution)/shard_map/ppermute | solution.py:198
  67.6 7.4 %collective-permute-start.22 = (bf16[64,896]{1,0:T(8,128)(2,1)S(1)}, bf16[64,896]{1,0:T(8,128)(2,1)S(1)}, u32[]{:S(2)}, u32[]{:S(2)}) collective-permute-start(bf16[64,896]{1,0:T(8,128)(2,1)S(1)} %collective-permute-done.21.refs_2_), channel_id=1, source_target_pairs={{0,4},{4,0},{8,12},{12,8},{16,20},{20,16},{24,28},{28,24},{1,5},{5... | collective-permute-start | bytes 344072 | tf_op jit(solution)/shard_map/ppermute | solution.py:198
  81.4 6.6 %collective-permute-start.32 = (bf16[192,256]{1,0:T(8,128)(2,1)S(1)}, bf16[192,256]{1,0:T(8,128)(2,1)S(1)}, u32[]{:S(2)}, u32[]{:S(2)}) collective-permute-start(bf16[192,256]{1,0:T(8,128)(2,1)S(1)} %shard_map.109.refs_0_), channel_id=1, source_target_pairs={{0,24},{4,28},{8,16},{12,20},{16,8},{20,12},{24,0},{28,4},{1,25},{... | collective-permute-start | bytes 294920 | tf_op jit(solution)/shard_map/ppermute | solution.py:198
  83.1 6.4 %collective-permute-start.30 = (bf16[192,256]{1,0:T(8,128)(2,1)S(1)}, bf16[192,256]{1,0:T(8,128)(2,1)S(1)}, u32[]{:S(2)}, u32[]{:S(2)}) collective-permute-start(bf16[192,256]{1,0:T(8,128)(2,1)S(1)} %shard_map.109.refs_0_), channel_id=1, source_target_pairs={{0,16},{4,20},{8,24},{12,28},{16,0},{20,4},{24,8},{28,12},{1,17},{... | collective-permute-start | bytes 294920 | tf_op jit(solution)/shard_map/ppermute | solution.py:198
  84.4 5.1 %collective-permute-start.28 = (bf16[192,256]{1,0:T(8,128)(2,1)S(1)}, bf16[192,256]{1,0:T(8,128)(2,1)S(1)}, u32[]{:S(2)}, u32[]{:S(2)}) collective-permute-start(bf16[192,256]{1,0:T(8,128)(2,1)S(1)} %shard_map.109.refs_0_), channel_id=1, source_target_pairs={{0,8},{4,12},{8,0},{12,4},{16,24},{20,28},{24,16},{28,20},{1,9},{5... | collective-permute-start | bytes 294920 | tf_op jit(solution)/shard_map/ppermute | solution.py:198
  84.9 9.3 %collective-permute-start.27 = (bf16[192,256]{1,0:T(8,128)(2,1)S(1)}, bf16[192,256]{1,0:T(8,128)(2,1)S(1)}, u32[]{:S(2)}, u32[]{:S(2)}) collective-permute-start(bf16[192,256]{1,0:T(8,128)(2,1)S(1)} %shard_map.109.refs_0_), channel_id=1, source_target_pairs={{0,4},{4,0},{8,12},{12,8},{16,20},{20,16},{24,28},{28,24},{1,5},{5... | collective-permute-start | bytes 294920 | tf_op jit(solution)/shard_map/ppermute | solution.py:198
  88.0 6.2 %collective-permute-start.33 = (bf16[192,256]{1,0:T(8,128)(2,1)S(1)}, bf16[192,256]{1,0:T(8,128)(2,1)S(1)}, u32[]{:S(2)}, u32[]{:S(2)}) collective-permute-start(bf16[192,256]{1,0:T(8,128)(2,1)S(1)} %collective-permute-done.32.refs_6_), channel_id=1, source_target_pairs={{0,4},{4,0},{8,12},{12,8},{16,20},{20,16},{24,28},{28,24},{1,5},{5... | collective-permute-start | bytes 294920 | tf_op jit(solution)/shard_map/ppermute | solution.py:198
  89.5 4.7 %collective-permute-start.31 = (bf16[192,256]{1,0:T(8,128)(2,1)S(1)}, bf16[192,256]{1,0:T(8,128)(2,1)S(1)}, u32[]{:S(2)}, u32[]{:S(2)}) collective-permute-start(bf16[192,256]{1,0:T(8,128)(2,1)S(1)} %collective-permute-done.30.refs_4_), channel_id=1, source_target_pairs={{0,4},{4,0},{8,12},{12,8},{16,20},{20,16},{24,28},{28,24},{1,5},{5... | collective-permute-start | bytes 294920 | tf_op jit(solution)/shard_map/ppermute | solution.py:198
  89.5 4.7 %collective-permute-start.29 = (bf16[192,256]{1,0:T(8,128)(2,1)S(1)}, bf16[192,256]{1,0:T(8,128)(2,1)S(1)}, u32[]{:S(2)}, u32[]{:S(2)}) collective-permute-start(bf16[192,256]{1,0:T(8,128)(2,1)S(1)} %collective-permute-done.28.refs_2_), channel_id=1, source_target_pairs={{0,4},{4,0},{8,12},{12,8},{16,20},{20,16},{24,28},{28,24},{1,5},{5... | collective-permute-start | bytes 294920 | tf_op jit(solution)/shard_map/ppermute | solution.py:198
  97.5 4.2 %collective-permute-start.34 = (bf16[16,896]{1,0:T(8,128)(2,1)S(1)}, bf16[16,896]{1,0:T(8,128)(2,1)S(1)}, u32[]{:S(2)}, u32[]{:S(2)}) collective-permute-start(bf16[16,896]{1,0:T(8,128)(2,1)S(1)} %get-tuple-element.22), channel_id=1, source_target_pairs={{0,1},{1,0},{2,3},{3,2},{4,5},{5,4},{6,7},{7,6},{8,9},{9,8},{10,11... | collective-permute-start | bytes 86024 | tf_op jit(solution)/shard_map/ppermute | solution.py:198
  99.9 5.7 %collective-permute-start.36 = (bf16[16,896]{1,0:T(8,128)(2,1)S(1)}, bf16[16,896]{1,0:T(8,128)(2,1)S(1)}, u32[]{:S(2)}, u32[]{:S(2)}) collective-permute-start(bf16[16,896]{1,0:T(8,128)(2,1)S(1)} %get-tuple-element.23), channel_id=1, source_target_pairs={{0,3},{1,2},{2,1},{3,0},{4,7},{5,6},{6,5},{7,4},{8,11},{9,10},{10,... | collective-permute-start | bytes 86024 | tf_op jit(solution)/shard_map/ppermute | solution.py:198
  101.5 4.8 %collective-permute-start.35 = (bf16[16,896]{1,0:T(8,128)(2,1)S(1)}, bf16[16,896]{1,0:T(8,128)(2,1)S(1)}, u32[]{:S(2)}, u32[]{:S(2)}) collective-permute-start(bf16[16,896]{1,0:T(8,128)(2,1)S(1)} %get-tuple-element.24), channel_id=1, source_target_pairs={{0,2},{1,3},{2,0},{3,1},{4,6},{5,7},{6,4},{7,5},{8,10},{9,11},{10,... | collective-permute-start | bytes 86024 | tf_op jit(solution)/shard_map/ppermute | solution.py:198
where the time goes:
time: 107 us
  Pallas kernels  43 us (40%)
  waiting for transfers between devices  30.4 us (28%)
  starting transfers between devices  29.6 us (28%)
  other arithmetic  2.95 us (3%)
    ppermute x37, waiting for transfers between devices, xor_permute(): return lax.ppermute(value, axis, [(i, i ^ bits) for i in range(size)])  30.4 us
    ppermute x37, starting transfers between devices, xor_permute(): return lax.ppermute(value, axis, [(i, i ^ bits) for i in range(size)])  29.6 us
    pallas_call x4, Pallas kernels, prefetch(): pl.pallas_call(functools.partial(prefetch_kernel, layer=layer, count=len(...  19.7 us
    pallas_call x2, Pallas kernels, fast_device(): pl.pallas_call(functools.partial(gate_kernel, layer=layer, top=top, rows=...  12.5 us
    pallas_call x2, Pallas kernels, fast_device(): pl.pallas_call(functools.partial(down_kernel, layer=layer, shards=shards,...  6.55 us
    pallas_call x1, Pallas kernels, fast_device(): mask, gains, gates = prepare(stream, *small)  4.25 us
  transfers between devices with their start and end apart: 37, of which 14 were waited for; matrix products, arithmetic and copies ran while one was open for 0% of the time, Pallas kernels for 22%

commit v1 on v0

--- a/solution.py
+++ b/solution.py
@@ -67,19 +67,58 @@
             mask_ref[layer, j] = jnp.dot(mask.astype(bf16), swap, preferred_element_type=f32)
 
 
+def slabs(source, target, ks, size, sems):
+    column = lax.axis_index("ep")
+    moves = []
+    for i, k in enumerate(ks):
+        block = pl.ds(pl.multiple_of((column ^ k) * size, lanes), size)
+        moves.append(pltpu.make_async_copy(source.at[:, :, block], target.at[:, :, block], sems.at[i]))
+    return moves
+
+
 def setup_kernel(
-    _, plan_hbm, route_hbm, pick_hbm, gain_hbm, weight_hbm, mask_ref, gain_ref, weight_ref, plan_ref, route_ref, pick_ref, sems, *, sizes
+    x_ref, ups_ref, plan_hbm, route_hbm, pick_hbm, gain_hbm, weight_hbm, mask_ref, gain_ref, weight_ref, sums_ref, total_ref,
+    plan_ref, route_ref, pick_ref, sems, slab_sems, *, sizes, shards, units, width,
 ):
-    small = [(plan_hbm, plan_ref), (route_hbm, route_ref), (pick_hbm, pick_ref), (gain_hbm, gain_ref)]
+    small = [(plan_hbm, plan_ref), (route_hbm, route_ref), (pick_hbm, pick_ref)]
+    small.append((gain_hbm, gain_ref.at[:, pl.ds(0, gain_hbm.shape[1])]))
     moves = [pltpu.make_async_copy(src, dst, sems.at[i]) for i, (src, dst) in enumerate(small)]
-    moves.append(pltpu.make_async_copy(weight_hbm.at[0], weight_ref, sems.at[len(small)]))
-    for move in moves:
+    heavy = slabs(weight_hbm.at[0], weight_ref, range(shards), width, slab_sems)
+    for move in moves + heavy:
         move.start()
     for move in moves[:3]:
         move.wait()
     routing(plan_ref, route_ref, pick_ref, mask_ref, sizes)
-    for move in moves[3:]:
+    moves[3].wait()
+    heavy[0].wait()
+    squares, sums = feature_sums((weight_ref, ups_ref), gain_ref, [x_ref], (0,), 0, sizes[4], units, width)
+    tokens = x_ref.shape[0]
+    for i, part in enumerate(sums):
+        sums_ref[i, :, :tokens] = part
+    total_ref[...] = jnp.broadcast_to(squares, (tokens, lanes))
+    for move in heavy[1:]:
         move.wait()
+
+
+def early_kernel(_, weight_hbm, result_ref, sems, *, ks, width):
+    moves = slabs(weight_hbm.at[0], result_ref, ks, width, sems)
+    for move in moves:
+        move.start()
+    for move in moves:
+        move.wait()
+
+
+def early(after, weight, ks, width):
+    return pl.pallas_call(
+        functools.partial(early_kernel, ks=ks, width=width),
+        out_shape=pltpu.VMEM(weight.shape[1:], weight.dtype),
+        in_specs=[any_spec(), hbm_spec()],
+        out_specs=vmem_spec(),
+        scratch_shapes=[pltpu.SemaphoreType.DMA((len(ks),))],
+        compiler_params=pltpu.CompilerParams(vmem_limit_bytes=2**20),
+        cost_estimate=pl.CostEstimate(flops=4 * 10**9, bytes_accessed=2 * 10**7, transcendentals=0),
+        name="early",
+    )(after, in_hbm(weight))
 
 
 def prefetch_kernel(*refs, layer, count):
@@ -93,41 +132,59 @@
         move.wait()
 
 
-def gate_kernel(mask_ref, num_ref, gain_ref, *refs, layer, top, rows, shards, exp_host, units, width):
-    x_refs = refs[:shards]
-    gate_ref, up_ref, out_ref, acc_ref = refs[shards:]
+def feature_sums(weight_refs, gain_ref, x_refs, ks, layer, exp_host, units, width):
     column = lax.axis_index("ep")
-    pairs = shards // 2
-    pair_width = 2 * width
-    full = shards * width
+    offsets = [pl.multiple_of((column ^ k) * width, lanes) for k in ks]
+    squares, scaled = 0.0, []
+    for x_ref, offset in zip(x_refs, offsets):
+        x = x_ref[...].astype(f32)
+        squares = squares + jnp.sum(x * x, axis=1, keepdims=True)
+        scaled.append((x * gain_ref[layer : layer + 1, pl.ds(offset, width)]).astype(bf16))
+    scaled = jnp.concatenate(scaled, axis=1)
+    sums = []
+    for weight_ref in weight_refs:
+        weight = jnp.concatenate([weight_ref[:, :, pl.ds(offset, width)] for offset in offsets], axis=2)
+        weight = weight.reshape(exp_host * units, len(ks) * width)
+        sums.append(lax.dot_general(weight, scaled, (((1,), (1,)), ((), ())), preferred_element_type=f32))
+    return squares, sums
+
+
+def gate_part(*refs, layer, ks, first, last, fill, top, rows, shards, exp_host, units, width):
+    refs = list(refs)
+    gate_ref, up_ref, gain_ref = refs[:3]
+    x_refs = refs[3 : 3 + len(ks)]
+    refs = refs[3 + len(ks) :]
+    moves = []
+    if not first:
+        sums_ref, squares_ref = refs[:2]
+        refs = refs[2:]
+    if fill:
+        source = refs.pop(0)
+        sems = refs.pop()
+        up_ref = refs.pop()
+        moves = slabs(source.at[layer], up_ref, fill, width, sems)
+        for move in moves:
+            move.start()
+    if last:
+        mask_ref, num_ref, out_ref, acc_ref = refs
+    else:
+        acc_ref, total_ref = refs
     tokens = x_refs[0].shape[0]
-    odd = column % 2 == 1
-    squares = jnp.zeros((tokens, 1), f32)
-    for m in range(pairs):
-        mine = x_refs[2 * m][...].astype(f32)
-        other = x_refs[2 * m + 1][...].astype(f32)
-        squares = squares + jnp.sum(mine * mine + other * other, axis=1, keepdims=True)
-        both = jnp.concatenate([jnp.where(odd, other, mine), jnp.where(odd, mine, other)], axis=1)
-        offset = pl.multiple_of(((column // 2) ^ m) * pair_width, lanes)
-        gain = gain_ref[layer : layer + 1, pl.ds(offset, pair_width)]
-        scaled = (both * gain).astype(bf16)
-        for i, weight_ref in enumerate((gate_ref, up_ref)):
-            part = lax.dot_general(
-                weight_ref[:, :, pl.ds(offset, pair_width)].reshape(exp_host * units, pair_width),
-                scaled,
-                (((1,), (1,)), ((), ())),
-                preferred_element_type=f32,
-            )
-            if m == 0:
-                acc_ref[i, :, :tokens] = part
-            else:
-                acc_ref[i, :, :tokens] = acc_ref[i, :, :tokens] + part
-    inverse = lax.rsqrt(squares / full + epsilon)
+    squares, sums = feature_sums((gate_ref, up_ref), gain_ref, x_refs, ks, layer, exp_host, units, width)
+    if not first:
+        squares = squares + squares_ref[:, 0:1]
+    for i, part in enumerate(sums):
+        acc_ref[i, :, :tokens] = part if first else sums_ref[i, :, :tokens] + part
+    for move in moves:
+        move.wait()
+    if not last:
+        total_ref[...] = jnp.broadcast_to(squares, (tokens, lanes))
+        return
+    inverse = lax.rsqrt(squares / (shards * width) + epsilon)
     turned = jnp.concatenate([jnp.broadcast_to(inverse, (tokens, lanes)), jnp.zeros((lanes - tokens, lanes), f32)], axis=0).T
     scale = turned[0:1, :]
-    blocks = num_ref.shape[0] // rows
     numbers = num_ref[0:rows, :].astype(f32)
-    for b in range(1, blocks):
+    for b in range(1, num_ref.shape[0] // rows):
         numbers = numbers + pltpu.roll(num_ref[b * rows : (b + 1) * rows, :].astype(f32), b * rows, 1)
     numbers = numbers[layer * top : (layer + 1) * top, :]
     shares = numbers / jnp.maximum(jnp.sum(numbers, axis=0, keepdims=True), 1.0)
@@ -139,30 +196,146 @@
         out_ref[j * tokens : (j + 1) * tokens, :] = hidden.T[:tokens].astype(bf16)
 
 
-def down_kernel(*refs, layer, shards, exp_host, units, width, tokens):
-    h_refs = refs[:shards]
-    down_ref, own_ref, send_ref, acc_ref = refs[shards:]
+def gate_up(layer, ks, gates, ups, gains, xs, sums, finish, sizes, units, width, shards, load=None, fill=()):
+    _, groups, rows, top, exp_host, _, _ = sizes
+    count = groups * rows
+    sums_shape = pltpu.VMEM((2, exp_host * units, lanes), f32)
+    last = finish is not None
+    operands = [gates, ups, gains] + [xs[k] for k in ks] + list(sums or ()) + list(finish or ())
+    in_specs = [vmem_spec()] * len(operands)
+    out_shape = [pltpu.VMEM((exp_host * count, units), bf16)] if last else [sums_shape, pltpu.VMEM((count, lanes), f32)]
+    scratch = [sums_shape] if last else []
+    aliases = {}
+    if load is not None:
+        operands.append(in_hbm(load))
+        in_specs.append(hbm_spec())
+        out_shape.append(pltpu.VMEM(load.shape[1:], load.dtype))
+        scratch.append(pltpu.SemaphoreType.DMA((len(fill),)))
+        aliases = {1: len(out_shape) - 1}
+    work = 2 * 2 * exp_host * units * width * len(ks) * count
+    return pl.pallas_call(
+        functools.partial(
+            gate_part,
+            layer=layer,
+            ks=ks,
+            first=sums is None,
+            last=last,
+            fill=fill,
+            top=top,
+            rows=rows,
+            shards=shards,
+            exp_host=exp_host,
+            units=units,
+            width=width,
+        ),
+        out_shape=out_shape,
+        in_specs=in_specs,
+        out_specs=[vmem_spec()] * len(out_shape),
+        scratch_shapes=scratch,
+        input_output_aliases=aliases,
+        compiler_params=pltpu.CompilerParams(vmem_limit_bytes=8 * 2**20),
+        cost_estimate=pl.CostEstimate(flops=work, bytes_accessed=work // count, transcendentals=0),
+    )(*operands)
+
+
+def down_part(*refs, ks, first, last, exp_host, units, tokens):
+    down_ref = refs[0]
+    h_refs = refs[1 : 1 + len(ks)]
+    refs = refs[1 + len(ks) :]
     column = lax.axis_index("ep")
-    pairs = shards // 2
-    pair_units = 2 * units
-    odd = column % 2 == 1
-    for m in range(pairs):
-        parts = []
+    parts, weights = [], []
+    for h_ref, k in zip(h_refs, ks):
+        offset = pl.multiple_of((column ^ k) * units, lanes)
         for j in range(exp_host):
-            mine = h_refs[2 * m][j * tokens : (j + 1) * tokens, :].astype(f32)
-            other = h_refs[2 * m + 1][j * tokens : (j + 1) * tokens, :].astype(f32)
-            parts += [jnp.where(odd, other, mine), jnp.where(odd, mine, other)]
-        hidden = jnp.concatenate(parts, axis=1).astype(bf16)
-        offset = pl.multiple_of(((column // 2) ^ m) * pair_units, lanes)
-        weights = jnp.concatenate([down_ref[j, :, pl.ds(offset, pair_units)] for j in range(exp_host)], axis=1)
-        part = lax.dot_general(weights, hidden, (((1,), (1,)), ((), ())), preferred_element_type=f32)
-        if m == 0:
-            acc_ref[:, :tokens] = part
-        else:
-            acc_ref[:, :tokens] = acc_ref[:, :tokens] + part
+            parts.append(h_ref[j * tokens : (j + 1) * tokens, :])
+            weights.append(down_ref[j, :, pl.ds(offset, units)])
+    part = lax.dot_general(
+        jnp.concatenate(weights, axis=1),
+        jnp.concatenate(parts, axis=1),
+        (((1,), (1,)), ((), ())),
+        preferred_element_type=f32,
+    )
+    if not first:
+        part = refs[0][:, :tokens] + part
+        refs = refs[1:]
+    if not last:
+        refs[0][:, :tokens] = part
+        return
+    own_ref, send_ref, acc_ref = refs
+    acc_ref[:, :tokens] = part
     result = acc_ref[...].T[:tokens]
     own_ref[...] = result
     send_ref[...] = result.astype(bf16)
+
+
+def down_first_kernel(h_ref, weight_hbm, weight_ref, sums_ref, sems, *, layer, shards, exp_host, units, tokens):
+    moves = slabs(weight_hbm.at[layer], weight_ref, range(shards), units, sems)
+    for move in moves:
+        move.start()
+    moves[0].wait()
+    down_part(weight_ref, h_ref, sums_ref, ks=(0,), first=True, last=False, exp_host=exp_host, units=units, tokens=tokens)
+    for move in moves[1:]:
+        move.wait()
+
+
+def down_first(layer, weight, hidden, shards, count, units, width, exp_host):
+    return pl.pallas_call(
+        functools.partial(
+            down_first_kernel, layer=layer, shards=shards, exp_host=exp_host, units=units, tokens=count
+        ),
+        out_shape=[pltpu.VMEM(weight.shape[1:], weight.dtype), pltpu.VMEM((width, lanes), f32)],
+        in_specs=[vmem_spec(), hbm_spec()],
+        out_specs=[vmem_spec()] * 2,
+        scratch_shapes=[pltpu.SemaphoreType.DMA((shards,))],
+        compiler_params=pltpu.CompilerParams(vmem_limit_bytes=8 * 2**20),
+        cost_estimate=pl.CostEstimate(flops=4 * 10**9, bytes_accessed=2 * 10**7, transcendentals=0),
+    )(hidden, in_hbm(weight))
+
+
+def down(ks, downs, hs, sums, last, count, units, width, exp_host):
+    sums_shape = pltpu.VMEM((width, lanes), f32)
+    operands = [downs] + [hs[k] for k in ks] + ([] if sums is None else [sums])
+    work = 2 * exp_host * units * width * len(ks) * count
+    return pl.pallas_call(
+        functools.partial(
+            down_part, ks=ks, first=sums is None, last=last, exp_host=exp_host, units=units, tokens=count
+        ),
+        out_shape=(pltpu.VMEM((count, width), f32), pltpu.VMEM((count, width), bf16)) if last else sums_shape,
+        in_specs=[vmem_spec()] * len(operands),
+        out_specs=(vmem_spec(), vmem_spec()) if last else vmem_spec(),
+        scratch_shapes=[sums_shape] if last else [],
+        compiler_params=pltpu.CompilerParams(vmem_limit_bytes=8 * 2**20),
+        cost_estimate=pl.CostEstimate(flops=work, bytes_accessed=work // count, transcendentals=0),
+    )(*operands)
+
+
+def pack_kernel(tokens_hbm, numbers_hbm, out_ref, numbers_ref, sems, *, width):
+    moves = [
+        pltpu.make_async_copy(numbers_hbm, numbers_ref, sems.at[0]),
+        pltpu.make_async_copy(tokens_hbm, out_ref.at[:, pl.ds(0, width)], sems.at[1]),
+    ]
+    for move in moves:
+        move.start()
+    layers, top, rows = numbers_ref.shape
+    out_ref[:, width:] = jnp.zeros((out_ref.shape[0], lanes), bf16)
+    moves[0].wait()
+    numbers = jnp.concatenate([numbers_ref[layer] for layer in range(layers)], axis=0)
+    out_ref[: layers * top, width : width + rows] = numbers.astype(f32).astype(bf16)
+    moves[1].wait()
+
+
+def pack(tokens, combine_num):
+    rows, width = tokens.shape
+    layers, _, top = combine_num.shape
+    return pl.pallas_call(
+        functools.partial(pack_kernel, width=width),
+        out_shape=pltpu.VMEM((rows, width + lanes), bf16),
+        in_specs=[hbm_spec()] * 2,
+        out_specs=vmem_spec(),
+        scratch_shapes=[pltpu.VMEM((layers, top, rows), jnp.int32), pltpu.SemaphoreType.DMA((2,))],
+        compiler_params=pltpu.CompilerParams(vmem_limit_bytes=2**20),
+        name="pack",
+    )(in_hbm(tokens), in_hbm(combine_num.transpose(0, 2, 1)))
 
 
 def vmem_spec():
@@ -221,11 +394,11 @@
     capacity = rows // 2
     sizes = (layers, groups, rows, top, exp_host, rep_host, capacity)
 
-    numbers = combine_num.transpose(0, 2, 1).reshape(layers * top, rows).astype(bf16)
-    numbers = jnp.pad(numbers, ((0, rows - layers * top), (0, lanes - rows)))
-    payload = jnp.concatenate([tokens, numbers], axis=1)
+    same = tuple(range(0, shards, 2))
+    late = tuple(k + 1 for k in same)
+    payload = pack(tokens, combine_num)
     gathered = [payload]
-    (ups,) = prefetch(0, payload, up_weight)
+    ups = early(payload, up_weight, same, width)
     for k in range(1, groups):
         gathered.append(xor_permute(payload, "dp", groups, k))
     gathered = jnp.concatenate(gathered, axis=0)
@@ -233,56 +406,47 @@
     number = gathered[:, width:]
 
     prepare = pl.pallas_call(
-        functools.partial(setup_kernel, sizes=sizes),
+        functools.partial(setup_kernel, sizes=sizes, shards=shards, units=units, width=width),
         out_shape=(
             pltpu.VMEM((layers, exp_host, top, lanes), f32),
-            pltpu.VMEM(norm_gain.shape, f32),
+            pltpu.VMEM((layers, norm_gain.shape[1] + 4 * lanes), f32),
             pltpu.VMEM(gate_weight.shape[1:], bf16),
+            pltpu.VMEM((2, exp_host * units, lanes), f32),
+            pltpu.VMEM((count, lanes), f32),
         ),
-        in_specs=[any_spec()] + [hbm_spec()] * 5,
-        out_specs=(vmem_spec(),) * 3,
+        in_specs=[vmem_spec()] * 2 + [hbm_spec()] * 5,
+        out_specs=(vmem_spec(),) * 5,
         scratch_shapes=[
             pltpu.SMEM((layers, rep_host, groups), jnp.int32),
             pltpu.VMEM((layers, top, count), jnp.int32),
             pltpu.VMEM((layers, top, count), jnp.int32),
-            pltpu.SemaphoreType.DMA((5,)),
+            pltpu.SemaphoreType.DMA((4,)),
+            pltpu.SemaphoreType.DMA((shards,)),
         ],
-        compiler_params=pltpu.CompilerParams(vmem_limit_bytes=4 * 2**20),
+        compiler_params=pltpu.CompilerParams(vmem_limit_bytes=8 * 2**20),
         cost_estimate=pl.CostEstimate(flops=4 * 10**9, bytes_accessed=2 * 10**7, transcendentals=0),
         name="setup",
     )
     small = (replica_plan, route_expert, replica_pick)
     small = [in_hbm(v.transpose(0, 2, 1)) for v in small] + [in_hbm(norm_gain), in_hbm(gate_weight)]
-    mask, gains, gates = prepare(stream, *small)
+    mask, gains, gates, *sums = prepare(stream, ups, *small)
 
     for layer in range(layers):
         xs = gather_shards(stream, shards)
-        hidden = pl.pallas_call(
-            functools.partial(
-                gate_kernel, layer=layer, top=top, rows=rows, shards=shards, exp_host=exp_host, units=units, width=width
-            ),
-            out_shape=jax.ShapeDtypeStruct((exp_host * count, units), bf16),
-            in_specs=[vmem_spec()] * (5 + shards),
-            out_specs=vmem_spec(),
-            scratch_shapes=[
-                pltpu.VMEM((2, exp_host * units, lanes), f32),
-            ],
-            compiler_params=pltpu.CompilerParams(vmem_limit_bytes=8 * 2**20),
-        )(mask, number, gains, *xs, gates, ups)
-        (downs,) = prefetch(layer, hidden, down_weight)
+        dims = (sizes, units, width, shards)
+        finish = (mask, number)
+        if layer == 0:
+            *sums, ups = gate_up(layer, same[1:], gates, ups, gains, xs, sums, None, *dims, load=up_weight, fill=late)
+            (hidden,) = gate_up(layer, late, gates, ups, gains, xs, sums, finish, *dims)
+        else:
+            sums = gate_up(layer, (0, 1), gates, ups, gains, xs, None, None, *dims)
+            sums = gate_up(layer, same[1:], gates, ups, gains, xs, sums, None, *dims)
+            (hidden,) = gate_up(layer, late[1:], gates, ups, gains, xs, sums, finish, *dims)
         hs = gather_shards(hidden, shards)
-        own, send = pl.pallas_call(
-            functools.partial(
-                down_kernel, layer=layer, shards=shards, exp_host=exp_host, units=units, width=width, tokens=count
-            ),
-            out_shape=(jax.ShapeDtypeStruct((count, width), f32), jax.ShapeDtypeStruct((count, width), bf16)),
-            in_specs=[vmem_spec()] * (shards + 1),
-            out_specs=(vmem_spec(), vmem_spec()),
-            scratch_shapes=[
-                pltpu.VMEM((width, lanes), f32),
-            ],
-            compiler_params=pltpu.CompilerParams(vmem_limit_bytes=8 * 2**20),
-        )(*hs, downs)
+        dims = (count, units, width, exp_host)
+        downs, sums = down_first(layer, down_weight, hidden, shards, *dims)
+        sums = down(same[1:], downs, hs, sums, False, *dims)
+        own, send = down(late, downs, hs, sums, True, *dims)
         if layer + 1 < layers:
             gates, ups = prefetch(layer + 1, send, gate_weight, up_weight)
             update = own
@@ -293,7 +457,8 @@
         else:
             update = own[:rows]
             for k in range(1, groups):
-                update = update + xor_permute(send[k * rows : (k + 1) * rows], "dp", groups, k).astype(f32)
+                other = xor_permute(send[k * rows : (k + 1) * rows], "dp", groups, k)
+                update = update + other.astype(f32)
             stream = stream[:rows]
         stream = (stream.astype(f32) + update).astype(bf16)
     return stream, update.astype(bf16)
@@ -363,7 +528,7 @@
     fits = (
         groups & (groups - 1) == 0
         and shards & (shards - 1) == 0
-        and 2 <= shards <= widest
+        and 4 <= shards <= widest
         and width % lanes == 0
         and units % lanes == 0
         and rows % 16 == 0

time: 107 us -> 103 us (0.963)
  other arithmetic: 2.95 us -> 0.74 us
    pallas_call x4 -> x1, Pallas kernels: 19.7 us -> 7.28 us  [prefetch(): pl.pallas_call(functools.partial(prefetch_kernel, layer=layer, count=len(...]
    pallas_call x5 -> x14, Pallas kernels: 23.3 us -> 35.1 us  [the longest x5 12.6 us: gate_up(): pl.pallas_call(functools.partial(gate_part, layer=layer, ks=ks, first=sum...]
  transfers between devices with their start and end apart: 37 -> 37, of which waited for: 14 -> 15; matrix products, arithmetic and copies ran while one was open for 0% -> 0% of each run, Pallas kernels for 22% -> 31%
where the time goes in v1:
time: 103 us
  Pallas kernels  42.4 us (41%)
  waiting for transfers between devices  29.6 us (29%)
  starting transfers between devices  29.4 us (29%)
    ppermute x37, waiting for transfers between devices, xor_permute(): return lax.ppermute(value, axis, [(i, i ^ bits) for i in range(size)])  29.6 us
    ppermute x37, starting transfers between devices, xor_permute(): return lax.ppermute(value, axis, [(i, i ^ bits) for i in range(size)])  29.4 us
    pallas_call x5, Pallas kernels, gate_up(): pl.pallas_call(functools.partial(gate_part, layer=layer, ks=ks, first=sum...  12.6 us
    pallas_call x2, Pallas kernels, down_first(): pl.pallas_call(functools.partial(down_first_kernel, layer=layer, shards=s...  8.7 us
    pallas_call x1, Pallas kernels, prefetch(): pl.pallas_call(functools.partial(prefetch_kernel, layer=layer, count=len(...  7.28 us
    pallas_call x4, Pallas kernels, down(): pl.pallas_call(functools.partial(down_part, ks=ks, first=sums is None, la...  6.01 us
    pallas_call x1, Pallas kernels, fast_device(): mask, gains, gates, *sums = prepare(stream, ups, *small)  4.36 us
    pallas_call x1, Pallas kernels, early(): pl.pallas_call(functools.partial(early_kernel, ks=ks, width=width), out_s...  2.63 us
  transfers between devices with their start and end apart: 37, of which 15 were waited for; matrix products, arithmetic and copies ran while one was open for 0% of the time, Pallas kernels for 31%

profile of v1, /device:TPU:0, one launch (start us, length us, event | category | flops | bytes accessed | tf_op | source)
XLA Modules:
  0.0 103.1 jit_solution(11498888610769418051)
XLA Ops:
  0.6 0.8 pack.1._
  1.4 3.1 %collective-permute-start = (bf16[16,1024]{1,0:T(8,128)(2,1)S(1)}, bf16[16,1024]{1,0:T(8,128)(2,1)S(1)}, u32[]{:S(2)}, u32[]{:S(2)}) collective-permute-start(bf16[16,1024]{1,0:T(8,128)(2,1)S(1)} %pack.1._), channel_id=1, source_target_pairs={{0,1},{1,0},{2,3},{3,2},{4,5},{5,4},{6,7},{7,6},{8,9},{9,8},{10,11... | collective-permute-start | bytes 98312 | tf_op jit(solution)/shard_map/ppermute | solution.py:371
  4.5 2.6 %collective-permute-start.1 = (bf16[16,1024]{1,0:T(8,128)(2,1)S(1)}, bf16[16,1024]{1,0:T(8,128)(2,1)S(1)}, u32[]{:S(2)}, u32[]{:S(2)}) collective-permute-start(bf16[16,1024]{1,0:T(8,128)(2,1)S(1)} %pack.1._), channel_id=1, source_target_pairs={{0,2},{1,3},{2,0},{3,1},{4,6},{5,7},{6,4},{7,5},{8,10},{9,11},{10,... | collective-permute-start | bytes 98312 | tf_op jit(solution)/shard_map/ppermute | solution.py:371
  7.1 2.6 %early.1.ups_ref.refs_1_ = bf16[3,256,7168]{2,1,0:T(8,128)(2,1)S(1)} custom-call(bf16[16,1024]{1,0:T(8,128)(2,1)S(1)} %pack.1._, bf16[2,3,256,7168]{3,2,1,0:T(8,128)(2,1)} %refs_2_.1), custom_call_target="tpu_custom_call" | custom-call | flops 4000000000 | bytes 20000000 | tf_op jit(solution)/shard_map/early/pallas_call | solution.py:112
  9.9 2.9 %collective-permute-done.2 = bf16[16,1024]{1,0:T(8,128)(2,1)S(1)} collective-permute-done((bf16[16,1024]{1,0:T(8,128)(2,1)S(1)}, bf16[16,1024]{1,0:T(8,128)(2,1)S(1)}, u32[]{:S(2)}, u32[]{:S(2)}) %collective-permute-start.2) | collective-permute-done | bytes 32800 | tf_op jit(solution)/shard_map/ppermute | solution.py:371
  12.9 1.6 %collective-permute-start.3 = (bf16[64,896]{1,0:T(8,128)(2,1)S(1)}, bf16[64,896]{1,0:T(8,128)(2,1)S(1)}, u32[]{:S(2)}, u32[]{:S(2)}) collective-permute-start(bf16[64,896]{1,0:T(8,128)(2,1)S(1)} %slice.72.x_ref), channel_id=1, source_target_pairs={{0,8},{4,12},{8,0},{12,4},{16,24},{20,28},{24,16},{28,20},{1,9},{5... | collective-permute-start | bytes 344072 | tf_op jit(solution)/shard_map/ppermute | solution.py:371
  14.4 1.5 %collective-permute-start.4 = (bf16[64,896]{1,0:T(8,128)(2,1)S(1)}, bf16[64,896]{1,0:T(8,128)(2,1)S(1)}, u32[]{:S(2)}, u32[]{:S(2)}) collective-permute-start(bf16[64,896]{1,0:T(8,128)(2,1)S(1)} %slice.72.x_ref), channel_id=1, source_target_pairs={{0,16},{4,20},{8,24},{12,28},{16,0},{20,4},{24,8},{28,12},{1,17},{... | collective-permute-start | bytes 344072 | tf_op jit(solution)/shard_map/ppermute | solution.py:371
  16.4 4.4 %setup.1 = (f32[2,3,8,128]{3,2,1,0:T(8,128)S(1)}, f32[2,7680]{1,0:T(2,128)S(1)}, bf16[3,256,7168]{2,1,0:T(8,128)(2,1)S(1)}, f32[2,768,128]{2,1,0:T(8,128)S(1)}, f32[64,128]{1,0:T(8,128)S(1)}) custom-call(bf16[64,896]{1,0:T(8,128)(2,1)S(1)} %slice.72.x_ref, bf16[3,256,7168]{2,1,0:T(8,128)(2,1)S(1)} %early.1.ups_ref.refs_1_, s32[2,2,4]{2,1,0:T(2,128)} %bitcast.7, ...), custom_call_target="tpu_custom_call" | custom-call | flops 4000000000 | bytes 20000000 | tf_op jit(solution)/shard_map/setup/pallas_call | solution.py:432
  20.8 0.6 collective-permute-start.7
  21.9 2.7 %shard_map.104 = (f32[2,768,128]{2,1,0:T(8,128)S(1)}, f32[64,128]{1,0:T(8,128)S(1)}, bf16[3,256,7168]{2,1,0:T(8,128)(2,1)S(1)}) custom-call(bf16[3,256,7168]{2,1,0:T(8,128)(2,1)S(1)} %get-tuple-element.24.refs_0_, bf16[3,256,7168]{2,1,0:T(8,128)(2,1)S(1)} %early.1.ups_ref.refs_1_, ...), custom_call_target="tpu_custom_call", output_to_operand_aliasing={{2}: (1, {})} | custom-call | flops 528482304 | bytes 8257536 | tf_op jit(solution)/shard_map/pallas_call | solution.py:216
  24.7 3.3 %shard_map.105.h_ref = bf16[192,256]{1,0:T(8,128)(2,1)S(1)} custom-call(bf16[3,256,7168]{2,1,0:T(8,128)(2,1)S(1)} %get-tuple-element.24.refs_0_, bf16[3,256,7168]{2,1,0:T(8,128)(2,1)S(1)} %get-tuple-element.28.refs_1_, f32[2,7680]{1,0:T(2,128)S(1)} %get-tuple-element.25.refs_2_, bf16[64,896]{1,0:T(8,128)(2,1)S(1)} %collective-permute-done.6.refs_3_, ...), custom_call_target="tpu_custom_call" | custom-call | flops 704643072 | bytes 11010048 | tf_op jit(solution)/shard_map/pallas_call | solution.py:216
  28.0 1.5 %collective-permute-start.11 = (bf16[192,256]{1,0:T(8,128)(2,1)S(1)}, bf16[192,256]{1,0:T(8,128)(2,1)S(1)}, u32[]{:S(2)}, u32[]{:S(2)}) collective-permute-start(bf16[192,256]{1,0:T(8,128)(2,1)S(1)} %shard_map.105.h_ref), channel_id=1, source_target_pairs={{0,8},{4,12},{8,0},{12,4},{16,24},{20,28},{24,16},{28,20},{1,9},{5... | collective-permute-start | bytes 294920 | tf_op jit(solution)/shard_map/ppermute | solution.py:371
  29.5 1.5 %collective-permute-start.13 = (bf16[192,256]{1,0:T(8,128)(2,1)S(1)}, bf16[192,256]{1,0:T(8,128)(2,1)S(1)}, u32[]{:S(2)}, u32[]{:S(2)}) collective-permute-start(bf16[192,256]{1,0:T(8,128)(2,1)S(1)} %shard_map.105.h_ref), channel_id=1, source_target_pairs={{0,16},{4,20},{8,24},{12,28},{16,0},{20,4},{24,8},{28,12},{1,17},{... | collective-permute-start | bytes 294920 | tf_op jit(solution)/shard_map/ppermute | solution.py:371
  31.1 0.5 collective-permute-start.15
  31.6 1.4 %collective-permute-done.11.refs_1_ = bf16[192,256]{1,0:T(8,128)(2,1)S(1)} collective-permute-done((bf16[192,256]{1,0:T(8,128)(2,1)S(1)}, bf16[192,256]{1,0:T(8,128)(2,1)S(1)}, u32[]{:S(2)}, u32[]{:S(2)}) %collective-permute-start.11) | collective-permute-done | bytes 98336 | tf_op jit(solution)/shard_map/ppermute | solution.py:371
  33.0 2.3 %collective-permute-done.13.refs_2_ = bf16[192,256]{1,0:T(8,128)(2,1)S(1)} collective-permute-done((bf16[192,256]{1,0:T(8,128)(2,1)S(1)}, bf16[192,256]{1,0:T(8,128)(2,1)S(1)}, u32[]{:S(2)}, u32[]{:S(2)}) %collective-permute-start.13) | collective-permute-done | bytes 98336 | tf_op jit(solution)/shard_map/ppermute | solution.py:371
  35.2 1.3 %collective-permute-done.15.refs_3_ = bf16[192,256]{1,0:T(8,128)(2,1)S(1)} collective-permute-done((bf16[192,256]{1,0:T(8,128)(2,1)S(1)}, bf16[192,256]{1,0:T(8,128)(2,1)S(1)}, u32[]{:S(2)}, u32[]{:S(2)}) %collective-permute-start.15) | collective-permute-done | bytes 98336 | tf_op jit(solution)/shard_map/ppermute | solution.py:371
  36.6 4.3 %shard_map.106 = (bf16[3,896,2048]{2,1,0:T(8,128)(2,1)S(1)}, f32[896,128]{1,0:T(8,128)S(1)}) custom-call(bf16[192,256]{1,0:T(8,128)(2,1)S(1)} %shard_map.105.h_ref, bf16[2,3,896,2048]{3,2,1,0:T(8,128)(2,1)} %weight_hbm.7), custom_call_target="tpu_custom_call" | custom-call | flops 4000000000 | bytes 20000000 | tf_op jit(solution)/shard_map/pallas_call | solution.py:282
  40.9 1.2 %shard_map.107.refs_5_ = f32[896,128]{1,0:T(8,128)S(1)} custom-call(bf16[3,896,2048]{2,1,0:T(8,128)(2,1)S(1)} %get-tuple-element.32.refs_0_, bf16[192,256]{1,0:T(8,128)(2,1)S(1)} %collective-permute-done.11.refs_1_, bf16[192,256]{1,0:T(8,128)(2,1)S(1)} %collective-permute-done.13.refs_2_, bf16[192,256]{1,0:T(8,128)(2,1)S(1)} %collective-permute-done.15.refs_3_, ...), custom_call_target="tpu_custom_call" | custom-call | flops 264241152 | bytes 4128768 | tf_op jit(solution)/shard_map/pallas_call | solution.py:299
  42.2 1.8 %shard_map.108 = (f32[64,896]{1,0:T(8,128)S(1)}, bf16[64,896]{1,0:T(8,128)(2,1)S(1)}) custom-call(bf16[3,896,2048]{2,1,0:T(8,128)(2,1)S(1)} %get-tuple-element.32.refs_0_, bf16[192,256]{1,0:T(8,128)(2,1)S(1)} %collective-permute-done.10.refs_1_, bf16[192,256]{1,0:T(8,128)(2,1)S(1)} %collective-permute-done.12.refs_2_, ...), custom_call_target="tpu_custom_call" | custom-call | flops 352321536 | bytes 5505024 | tf_op jit(solution)/shard_map/pallas_call | solution.py:299
  44.1 1.3 %collective-permute-start.19 = (bf16[64,896]{1,0:T(8,128)(2,1)S(1)}, bf16[64,896]{1,0:T(8,128)(2,1)S(1)}, u32[]{:S(2)}, u32[]{:S(2)}) collective-permute-start(bf16[64,896]{1,0:T(8,128)(2,1)S(1)} %get-tuple-element.35.refs_0_), channel_id=1, source_target_pairs={{0,3},{1,2},{2,1},{3,0},{4,7},{5,6},{6,5},{7,4},{8,11},{9,10},{10,... | collective-permute-start | bytes 344072 | tf_op jit(solution)/shard_map/ppermute | solution.py:371
  45.4 2.1 %collective-permute-start.17 = (bf16[64,896]{1,0:T(8,128)(2,1)S(1)}, bf16[64,896]{1,0:T(8,128)(2,1)S(1)}, u32[]{:S(2)}, u32[]{:S(2)}) collective-permute-start(bf16[64,896]{1,0:T(8,128)(2,1)S(1)} %get-tuple-element.35.refs_0_), channel_id=1, source_target_pairs={{0,1},{1,0},{2,3},{3,2},{4,5},{5,4},{6,7},{7,6},{8,9},{9,8},{10,11... | collective-permute-start | bytes 344072 | tf_op jit(solution)/shard_map/ppermute | solution.py:371
  47.6 6.4 %collective-permute-done.18 = bf16[64,896]{1,0:T(8,128)(2,1)S(1)} collective-permute-done((bf16[64,896]{1,0:T(8,128)(2,1)S(1)}, bf16[64,896]{1,0:T(8,128)(2,1)S(1)}, u32[]{:S(2)}, u32[]{:S(2)}) %collective-permute-start.18) | collective-permute-done | bytes 114720 | tf_op jit(solution)/shard_map/ppermute | solution.py:371
  54.0 1.7 %collective-permute-done.17 = bf16[64,896]{1,0:T(8,128)(2,1)S(1)} collective-permute-done((bf16[64,896]{1,0:T(8,128)(2,1)S(1)}, bf16[64,896]{1,0:T(8,128)(2,1)S(1)}, u32[]{:S(2)}, u32[]{:S(2)}) %collective-permute-start.17) | collective-permute-done | bytes 114720 | tf_op jit(solution)/shard_map/ppermute | solution.py:371
  55.8 0.8 collective-permute-start.20
  56.6 1.0 %collective-permute-start.22 = (bf16[64,896]{1,0:T(8,128)(2,1)S(1)}, bf16[64,896]{1,0:T(8,128)(2,1)S(1)}, u32[]{:S(2)}, u32[]{:S(2)}) collective-permute-start(bf16[64,896]{1,0:T(8,128)(2,1)S(1)} %fusion.3.refs_3_), channel_id=1, source_target_pairs={{0,16},{4,20},{8,24},{12,28},{16,0},{20,4},{24,8},{28,12},{1,17},{... | collective-permute-start | bytes 344072 | tf_op jit(solution)/shard_map/ppermute | solution.py:371
  57.7 1.7 %collective-permute-start.24 = (bf16[64,896]{1,0:T(8,128)(2,1)S(1)}, bf16[64,896]{1,0:T(8,128)(2,1)S(1)}, u32[]{:S(2)}, u32[]{:S(2)}) collective-permute-start(bf16[64,896]{1,0:T(8,128)(2,1)S(1)} %fusion.3.refs_3_), channel_id=1, source_target_pairs={{0,24},{4,28},{8,16},{12,20},{16,8},{20,12},{24,0},{28,4},{1,25},{... | collective-permute-start | bytes 344072 | tf_op jit(solution)/shard_map/ppermute | solution.py:371
  59.3 2.4 %collective-permute-done.20.refs_3_ = bf16[64,896]{1,0:T(8,128)(2,1)S(1)} collective-permute-done((bf16[64,896]{1,0:T(8,128)(2,1)S(1)}, bf16[64,896]{1,0:T(8,128)(2,1)S(1)}, u32[]{:S(2)}, u32[]{:S(2)}) %collective-permute-start.20) | collective-permute-done | bytes 114720 | tf_op jit(solution)/shard_map/ppermute | solution.py:371
  61.7 0.8 collective-permute-done.22.refs_4_
  62.6 1.2 %collective-permute-done.24.refs_5_ = bf16[64,896]{1,0:T(8,128)(2,1)S(1)} collective-permute-done((bf16[64,896]{1,0:T(8,128)(2,1)S(1)}, bf16[64,896]{1,0:T(8,128)(2,1)S(1)}, u32[]{:S(2)}, u32[]{:S(2)}) %collective-permute-start.24) | collective-permute-done | bytes 114720 | tf_op jit(solution)/shard_map/ppermute | solution.py:371
  63.8 7.3 %shard_map.109 = (bf16[3,256,7168]{2,1,0:T(8,128)(2,1)S(1)}, bf16[3,256,7168]{2,1,0:T(8,128)(2,1)S(1)}) custom-call(bf16[64,896]{1,0:T(8,128)(2,1)S(1)} %get-tuple-element.35.refs_0_, bf16[2,3,256,7168]{3,2,1,0:T(8,128)(2,1)} %refs_1_.1, bf16[2,3,256,7168]{3,2,1,0:T(8,128)(2,1)} %refs_2_.1), custom_call_target="tpu_custom_call" | custom-call | flops 8808038400 | bytes 44040192 | tf_op jit(solution)/shard_map/pallas_call | solution.py:359
  71.1 1.8 %shard_map.110 = (f32[2,768,128]{2,1,0:T(8,128)S(1)}, f32[64,128]{1,0:T(8,128)S(1)}) custom-call(bf16[3,256,7168]{2,1,0:T(8,128)(2,1)S(1)} %get-tuple-element.36.refs_0_, bf16[3,256,7168]{2,1,0:T(8,128)(2,1)S(1)} %get-tuple-element.37.refs_1_, f32[2,7680]{1,0:T(2,128)S(1)} %get-tuple-element.25.refs_2_, bf16[64,896]{1,0:T(8,128)(2,1)S(1)} %fusion.3.refs_3_, ...), custom_call_target="tpu_custom_call" | custom-call | flops 352321536 | bytes 5505024 | tf_op jit(solution)/shard_map/pallas_call | solution.py:216
  72.8 2.3 %shard_map.111 = (f32[2,768,128]{2,1,0:T(8,128)S(1)}, f32[64,128]{1,0:T(8,128)S(1)}) custom-call(bf16[3,256,7168]{2,1,0:T(8,128)(2,1)S(1)} %get-tuple-element.36.refs_0_, bf16[3,256,7168]{2,1,0:T(8,128)(2,1)S(1)} %get-tuple-element.37.refs_1_, f32[2,7680]{1,0:T(2,128)S(1)} %get-tuple-element.25.refs_2_, bf16[64,896]{1,0:T(8,128)(2,1)S(1)} %collective-permute-done.20.refs_3_, ...), custom_call_target="tpu_custom_call" | custom-call | flops 528482304 | bytes 8257536 | tf_op jit(solution)/shard_map/pallas_call | solution.py:216
  75.2 2.4 %shard_map.112.h_ref = bf16[192,256]{1,0:T(8,128)(2,1)S(1)} custom-call(bf16[3,256,7168]{2,1,0:T(8,128)(2,1)S(1)} %get-tuple-element.36.refs_0_, bf16[3,256,7168]{2,1,0:T(8,128)(2,1)S(1)} %get-tuple-element.37.refs_1_, f32[2,7680]{1,0:T(2,128)S(1)} %get-tuple-element.25.refs_2_, bf16[64,896]{1,0:T(8,128)(2,1)S(1)} %collective-permute-done.21.refs_3_, ...), custom_call_target="tpu_custom_call" | custom-call | flops 528482304 | bytes 8257536 | tf_op jit(solution)/shard_map/pallas_call | solution.py:216
  77.7 1.9 %collective-permute-start.28 = (bf16[192,256]{1,0:T(8,128)(2,1)S(1)}, bf16[192,256]{1,0:T(8,128)(2,1)S(1)}, u32[]{:S(2)}, u32[]{:S(2)}) collective-permute-start(bf16[192,256]{1,0:T(8,128)(2,1)S(1)} %shard_map.112.h_ref), channel_id=1, source_target_pairs={{0,8},{4,12},{8,0},{12,4},{16,24},{20,28},{24,16},{28,20},{1,9},{5... | collective-permute-start | bytes 294920 | tf_op jit(solution)/shard_map/ppermute | solution.py:371
  79.5 1.0 collective-permute-start.30
  80.6 0.6 collective-permute-start.32
  81.2 1.7 %collective-permute-done.28.refs_1_ = bf16[192,256]{1,0:T(8,128)(2,1)S(1)} collective-permute-done((bf16[192,256]{1,0:T(8,128)(2,1)S(1)}, bf16[192,256]{1,0:T(8,128)(2,1)S(1)}, u32[]{:S(2)}, u32[]{:S(2)}) %collective-permute-start.28) | collective-permute-done | bytes 98336 | tf_op jit(solution)/shard_map/ppermute | solution.py:371
  82.9 3.3 %collective-permute-done.30.refs_2_ = bf16[192,256]{1,0:T(8,128)(2,1)S(1)} collective-permute-done((bf16[192,256]{1,0:T(8,128)(2,1)S(1)}, bf16[192,256]{1,0:T(8,128)(2,1)S(1)}, u32[]{:S(2)}, u32[]{:S(2)}) %collective-permute-start.30) | collective-permute-done | bytes 98336 | tf_op jit(solution)/shard_map/ppermute | solution.py:371
  86.8 4.3 %shard_map.113 = (bf16[3,896,2048]{2,1,0:T(8,128)(2,1)S(1)}, f32[896,128]{1,0:T(8,128)S(1)}) custom-call(bf16[192,256]{1,0:T(8,128)(2,1)S(1)} %shard_map.112.h_ref, bf16[2,3,896,2048]{3,2,1,0:T(8,128)(2,1)} %weight_hbm.7), custom_call_target="tpu_custom_call" | custom-call | flops 4000000000 | bytes 20000000 | tf_op jit(solution)/shard_map/pallas_call | solution.py:282
  91.1 1.2 %shard_map.114.refs_5_ = f32[896,128]{1,0:T(8,128)S(1)} custom-call(bf16[3,896,2048]{2,1,0:T(8,128)(2,1)S(1)} %get-tuple-element.42.refs_0_, bf16[192,256]{1,0:T(8,128)(2,1)S(1)} %collective-permute-done.28.refs_1_, bf16[192,256]{1,0:T(8,128)(2,1)S(1)} %collective-permute-done.30.refs_2_, bf16[192,256]{1,0:T(8,128)(2,1)S(1)} %collective-permute-done.32.refs_3_, ...), custom_call_target="tpu_custom_call" | custom-call | flops 264241152 | bytes 4128768 | tf_op jit(solution)/shard_map/pallas_call | solution.py:299
  92.4 1.8 %shard_map.115 = (f32[64,896]{1,0:T(8,128)S(1)}, bf16[64,896]{1,0:T(8,128)(2,1)S(1)}) custom-call(bf16[3,896,2048]{2,1,0:T(8,128)(2,1)S(1)} %get-tuple-element.42.refs_0_, bf16[192,256]{1,0:T(8,128)(2,1)S(1)} %collective-permute-done.27.refs_1_, bf16[192,256]{1,0:T(8,128)(2,1)S(1)} %collective-permute-done.29.refs_2_, ...), custom_call_target="tpu_custom_call" | custom-call | flops 352321536 | bytes 5505024 | tf_op jit(solution)/shard_map/pallas_call | solution.py:299
  94.2 1.4 %collective-permute-start.34 = (bf16[16,896]{1,0:T(8,128)(2,1)S(1)}, bf16[16,896]{1,0:T(8,128)(2,1)S(1)}, u32[]{:S(2)}, u32[]{:S(2)}) collective-permute-start(bf16[16,896]{1,0:T(8,128)(2,1)S(1)} %get-tuple-element.48), channel_id=1, source_target_pairs={{0,1},{1,0},{2,3},{3,2},{4,5},{5,4},{6,7},{7,6},{8,9},{9,8},{10,11... | collective-permute-start | bytes 86024 | tf_op jit(solution)/shard_map/ppermute | solution.py:371
  95.6 1.1 %collective-permute-start.35 = (bf16[16,896]{1,0:T(8,128)(2,1)S(1)}, bf16[16,896]{1,0:T(8,128)(2,1)S(1)}, u32[]{:S(2)}, u32[]{:S(2)}) collective-permute-start(bf16[16,896]{1,0:T(8,128)(2,1)S(1)} %get-tuple-element.50), channel_id=1, source_target_pairs={{0,2},{1,3},{2,0},{3,1},{4,6},{5,7},{6,4},{7,5},{8,10},{9,11},{10,... | collective-permute-start | bytes 86024 | tf_op jit(solution)/shard_map/ppermute | solution.py:371
  96.8 1.9 %collective-permute-start.36 = (bf16[16,896]{1,0:T(8,128)(2,1)S(1)}, bf16[16,896]{1,0:T(8,128)(2,1)S(1)}, u32[]{:S(2)}, u32[]{:S(2)}) collective-permute-start(bf16[16,896]{1,0:T(8,128)(2,1)S(1)} %get-tuple-element.49), channel_id=1, source_target_pairs={{0,3},{1,2},{2,1},{3,0},{4,7},{5,6},{6,5},{7,4},{8,11},{9,10},{10,... | collective-permute-start | bytes 86024 | tf_op jit(solution)/shard_map/ppermute | solution.py:371
  98.7 2.5 %collective-permute-done.35 = bf16[16,896]{1,0:T(8,128)(2,1)S(1)} collective-permute-done((bf16[16,896]{1,0:T(8,128)(2,1)S(1)}, bf16[16,896]{1,0:T(8,128)(2,1)S(1)}, u32[]{:S(2)}, u32[]{:S(2)}) %collective-permute-start.35) | collective-permute-done | bytes 28704 | tf_op jit(solution)/shard_map/ppermute | solution.py:371
  101.2 1.2 %collective-permute-done.36 = bf16[16,896]{1,0:T(8,128)(2,1)S(1)} collective-permute-done((bf16[16,896]{1,0:T(8,128)(2,1)S(1)}, bf16[16,896]{1,0:T(8,128)(2,1)S(1)}, u32[]{:S(2)}, u32[]{:S(2)}) %collective-permute-start.36) | collective-permute-done | bytes 28704 | tf_op jit(solution)/shard_map/ppermute | solution.py:371
  102.4 0.6 fusion.4
  (50 shorter events, 2.0 us)
Async XLA Ops:
  1.4 8.4 %collective-permute-start = (bf16[16,1024]{1,0:T(8,128)(2,1)S(1)}, bf16[16,1024]{1,0:T(8,128)(2,1)S(1)}, u32[]{:S(2)}, u32[]{:S(2)}) collective-permute-start(bf16[16,1024]{1,0:T(8,128)(2,1)S(1)} %pack.1._), channel_id=1, source_target_pairs={{0,1},{1,0},{2,3},{3,2},{4,5},{5,4},{6,7},{7,6},{8,9},{9,8},{10,11... | collective-permute-start | bytes 98312 | tf_op jit(solution)/shard_map/ppermute | solution.py:371
  4.5 5.4 %collective-permute-start.1 = (bf16[16,1024]{1,0:T(8,128)(2,1)S(1)}, bf16[16,1024]{1,0:T(8,128)(2,1)S(1)}, u32[]{:S(2)}, u32[]{:S(2)}) collective-permute-start(bf16[16,1024]{1,0:T(8,128)(2,1)S(1)} %pack.1._), channel_id=1, source_target_pairs={{0,2},{1,3},{2,0},{3,1},{4,6},{5,7},{6,4},{7,5},{8,10},{9,11},{10,... | collective-permute-start | bytes 98312 | tf_op jit(solution)/shard_map/ppermute | solution.py:371
  7.1 5.7 %collective-permute-start.2 = (bf16[16,1024]{1,0:T(8,128)(2,1)S(1)}, bf16[16,1024]{1,0:T(8,128)(2,1)S(1)}, u32[]{:S(2)}, u32[]{:S(2)}) collective-permute-start(bf16[16,1024]{1,0:T(8,128)(2,1)S(1)} %pack.1._), channel_id=1, source_target_pairs={{0,3},{1,2},{2,1},{3,0},{4,7},{5,6},{6,5},{7,4},{8,11},{9,10},{10,... | collective-permute-start | bytes 98312 | tf_op jit(solution)/shard_map/ppermute | solution.py:371
  12.9 7.9 %collective-permute-start.3 = (bf16[64,896]{1,0:T(8,128)(2,1)S(1)}, bf16[64,896]{1,0:T(8,128)(2,1)S(1)}, u32[]{:S(2)}, u32[]{:S(2)}) collective-permute-start(bf16[64,896]{1,0:T(8,128)(2,1)S(1)} %slice.72.x_ref), channel_id=1, source_target_pairs={{0,8},{4,12},{8,0},{12,4},{16,24},{20,28},{24,16},{28,20},{1,9},{5... | collective-permute-start | bytes 344072 | tf_op jit(solution)/shard_map/ppermute | solution.py:371
  14.4 7.0 %collective-permute-start.4 = (bf16[64,896]{1,0:T(8,128)(2,1)S(1)}, bf16[64,896]{1,0:T(8,128)(2,1)S(1)}, u32[]{:S(2)}, u32[]{:S(2)}) collective-permute-start(bf16[64,896]{1,0:T(8,128)(2,1)S(1)} %slice.72.x_ref), channel_id=1, source_target_pairs={{0,16},{4,20},{8,24},{12,28},{16,0},{20,4},{24,8},{28,12},{1,17},{... | collective-permute-start | bytes 344072 | tf_op jit(solution)/shard_map/ppermute | solution.py:371
  15.9 5.7 %collective-permute-start.5 = (bf16[64,896]{1,0:T(8,128)(2,1)S(1)}, bf16[64,896]{1,0:T(8,128)(2,1)S(1)}, u32[]{:S(2)}, u32[]{:S(2)}) collective-permute-start(bf16[64,896]{1,0:T(8,128)(2,1)S(1)} %slice.72.x_ref), channel_id=1, source_target_pairs={{0,24},{4,28},{8,16},{12,20},{16,8},{20,12},{24,0},{28,4},{1,25},{... | collective-permute-start | bytes 344072 | tf_op jit(solution)/shard_map/ppermute | solution.py:371
  16.4 8.2 %collective-permute-start.6 = (bf16[64,896]{1,0:T(8,128)(2,1)S(1)}, bf16[64,896]{1,0:T(8,128)(2,1)S(1)}, u32[]{:S(2)}, u32[]{:S(2)}) collective-permute-start(bf16[64,896]{1,0:T(8,128)(2,1)S(1)} %slice.72.x_ref), channel_id=1, source_target_pairs={{0,4},{4,0},{8,12},{12,8},{16,20},{20,16},{24,28},{28,24},{1,5},{5... | collective-permute-start | bytes 344072 | tf_op jit(solution)/shard_map/ppermute | solution.py:371
  20.8 3.8 %collective-permute-start.7 = (bf16[64,896]{1,0:T(8,128)(2,1)S(1)}, bf16[64,896]{1,0:T(8,128)(2,1)S(1)}, u32[]{:S(2)}, u32[]{:S(2)}) collective-permute-start(bf16[64,896]{1,0:T(8,128)(2,1)S(1)} %collective-permute-done.3.refs_3_), channel_id=1, source_target_pairs={{0,4},{4,0},{8,12},{12,8},{16,20},{20,16},{24,28},{28,24},{1,5},{5... | collective-permute-start | bytes 344072 | tf_op jit(solution)/shard_map/ppermute | solution.py:371
  21.4 3.3 %collective-permute-start.8 = (bf16[64,896]{1,0:T(8,128)(2,1)S(1)}, bf16[64,896]{1,0:T(8,128)(2,1)S(1)}, u32[]{:S(2)}, u32[]{:S(2)}) collective-permute-start(bf16[64,896]{1,0:T(8,128)(2,1)S(1)} %collective-permute-done.4.refs_4_), channel_id=1, source_target_pairs={{0,4},{4,0},{8,12},{12,8},{16,20},{20,16},{24,28},{28,24},{1,5},{5... | collective-permute-start | bytes 344072 | tf_op jit(solution)/shard_map/ppermute | solution.py:371
  21.6 3.0 %collective-permute-start.9 = (bf16[64,896]{1,0:T(8,128)(2,1)S(1)}, bf16[64,896]{1,0:T(8,128)(2,1)S(1)}, u32[]{:S(2)}, u32[]{:S(2)}) collective-permute-start(bf16[64,896]{1,0:T(8,128)(2,1)S(1)} %collective-permute-done.5.refs_5_), channel_id=1, source_target_pairs={{0,4},{4,0},{8,12},{12,8},{16,20},{20,16},{24,28},{28,24},{1,5},{5... | collective-permute-start | bytes 344072 | tf_op jit(solution)/shard_map/ppermute | solution.py:371
  28.0 4.9 %collective-permute-start.11 = (bf16[192,256]{1,0:T(8,128)(2,1)S(1)}, bf16[192,256]{1,0:T(8,128)(2,1)S(1)}, u32[]{:S(2)}, u32[]{:S(2)}) collective-permute-start(bf16[192,256]{1,0:T(8,128)(2,1)S(1)} %shard_map.105.h_ref), channel_id=1, source_target_pairs={{0,8},{4,12},{8,0},{12,4},{16,24},{20,28},{24,16},{28,20},{1,9},{5... | collective-permute-start | bytes 294920 | tf_op jit(solution)/shard_map/ppermute | solution.py:371
  29.5 5.7 %collective-permute-start.13 = (bf16[192,256]{1,0:T(8,128)(2,1)S(1)}, bf16[192,256]{1,0:T(8,128)(2,1)S(1)}, u32[]{:S(2)}, u32[]{:S(2)}) collective-permute-start(bf16[192,256]{1,0:T(8,128)(2,1)S(1)} %shard_map.105.h_ref), channel_id=1, source_target_pairs={{0,16},{4,20},{8,24},{12,28},{16,0},{20,4},{24,8},{28,12},{1,17},{... | collective-permute-start | bytes 294920 | tf_op jit(solution)/shard_map/ppermute | solution.py:371
  31.1 5.5 %collective-permute-start.15 = (bf16[192,256]{1,0:T(8,128)(2,1)S(1)}, bf16[192,256]{1,0:T(8,128)(2,1)S(1)}, u32[]{:S(2)}, u32[]{:S(2)}) collective-permute-start(bf16[192,256]{1,0:T(8,128)(2,1)S(1)} %shard_map.105.h_ref), channel_id=1, source_target_pairs={{0,24},{4,28},{8,16},{12,20},{16,8},{20,12},{24,0},{28,4},{1,25},{... | collective-permute-start | bytes 294920 | tf_op jit(solution)/shard_map/ppermute | solution.py:371
  31.6 10.6 %collective-permute-start.10 = (bf16[192,256]{1,0:T(8,128)(2,1)S(1)}, bf16[192,256]{1,0:T(8,128)(2,1)S(1)}, u32[]{:S(2)}, u32[]{:S(2)}) collective-permute-start(bf16[192,256]{1,0:T(8,128)(2,1)S(1)} %shard_map.105.h_ref), channel_id=1, source_target_pairs={{0,4},{4,0},{8,12},{12,8},{16,20},{20,16},{24,28},{28,24},{1,5},{5... | collective-permute-start | bytes 294920 | tf_op jit(solution)/shard_map/ppermute | solution.py:371
  33.0 9.2 %collective-permute-start.12 = (bf16[192,256]{1,0:T(8,128)(2,1)S(1)}, bf16[192,256]{1,0:T(8,128)(2,1)S(1)}, u32[]{:S(2)}, u32[]{:S(2)}) collective-permute-start(bf16[192,256]{1,0:T(8,128)(2,1)S(1)} %collective-permute-done.11.refs_1_), channel_id=1, source_target_pairs={{0,4},{4,0},{8,12},{12,8},{16,20},{20,16},{24,28},{28,24},{1,5},{5... | collective-permute-start | bytes 294920 | tf_op jit(solution)/shard_map/ppermute | solution.py:371
  35.2 7.0 %collective-permute-start.14 = (bf16[192,256]{1,0:T(8,128)(2,1)S(1)}, bf16[192,256]{1,0:T(8,128)(2,1)S(1)}, u32[]{:S(2)}, u32[]{:S(2)}) collective-permute-start(bf16[192,256]{1,0:T(8,128)(2,1)S(1)} %collective-permute-done.13.refs_2_), channel_id=1, source_target_pairs={{0,4},{4,0},{8,12},{12,8},{16,20},{20,16},{24,28},{28,24},{1,5},{5... | collective-permute-start | bytes 294920 | tf_op jit(solution)/shard_map/ppermute | solution.py:371
  36.6 5.6 %collective-permute-start.16 = (bf16[192,256]{1,0:T(8,128)(2,1)S(1)}, bf16[192,256]{1,0:T(8,128)(2,1)S(1)}, u32[]{:S(2)}, u32[]{:S(2)}) collective-permute-start(bf16[192,256]{1,0:T(8,128)(2,1)S(1)} %collective-permute-done.15.refs_3_), channel_id=1, source_target_pairs={{0,4},{4,0},{8,12},{12,8},{16,20},{20,16},{24,28},{28,24},{1,5},{5... | collective-permute-start | bytes 294920 | tf_op jit(solution)/shard_map/ppermute | solution.py:371
  44.0 10.0 %collective-permute-start.18 = (bf16[64,896]{1,0:T(8,128)(2,1)S(1)}, bf16[64,896]{1,0:T(8,128)(2,1)S(1)}, u32[]{:S(2)}, u32[]{:S(2)}) collective-permute-start(bf16[64,896]{1,0:T(8,128)(2,1)S(1)} %get-tuple-element.35.refs_0_), channel_id=1, source_target_pairs={{0,2},{1,3},{2,0},{3,1},{4,6},{5,7},{6,4},{7,5},{8,10},{9,11},{10,... | collective-permute-start | bytes 344072 | tf_op jit(solution)/shard_map/ppermute | solution.py:371
  44.1 9.9 %collective-permute-start.19 = (bf16[64,896]{1,0:T(8,128)(2,1)S(1)}, bf16[64,896]{1,0:T(8,128)(2,1)S(1)}, u32[]{:S(2)}, u32[]{:S(2)}) collective-permute-start(bf16[64,896]{1,0:T(8,128)(2,1)S(1)} %get-tuple-element.35.refs_0_), channel_id=1, source_target_pairs={{0,3},{1,2},{2,1},{3,0},{4,7},{5,6},{6,5},{7,4},{8,11},{9,10},{10,... | collective-permute-start | bytes 344072 | tf_op jit(solution)/shard_map/ppermute | solution.py:371
  45.4 10.3 %collective-permute-start.17 = (bf16[64,896]{1,0:T(8,128)(2,1)S(1)}, bf16[64,896]{1,0:T(8,128)(2,1)S(1)}, u32[]{:S(2)}, u32[]{:S(2)}) collective-permute-start(bf16[64,896]{1,0:T(8,128)(2,1)S(1)} %get-tuple-element.35.refs_0_), channel_id=1, source_target_pairs={{0,1},{1,0},{2,3},{3,2},{4,5},{5,4},{6,7},{7,6},{8,9},{9,8},{10,11... | collective-permute-start | bytes 344072 | tf_op jit(solution)/shard_map/ppermute | solution.py:371
  55.8 5.9 %collective-permute-start.20 = (bf16[64,896]{1,0:T(8,128)(2,1)S(1)}, bf16[64,896]{1,0:T(8,128)(2,1)S(1)}, u32[]{:S(2)}, u32[]{:S(2)}) collective-permute-start(bf16[64,896]{1,0:T(8,128)(2,1)S(1)} %fusion.3.refs_3_), channel_id=1, source_target_pairs={{0,8},{4,12},{8,0},{12,4},{16,24},{20,28},{24,16},{28,20},{1,9},{5... | collective-permute-start | bytes 344072 | tf_op jit(solution)/shard_map/ppermute | solution.py:371
  56.6 5.9 %collective-permute-start.22 = (bf16[64,896]{1,0:T(8,128)(2,1)S(1)}, bf16[64,896]{1,0:T(8,128)(2,1)S(1)}, u32[]{:S(2)}, u32[]{:S(2)}) collective-permute-start(bf16[64,896]{1,0:T(8,128)(2,1)S(1)} %fusion.3.refs_3_), channel_id=1, source_target_pairs={{0,16},{4,20},{8,24},{12,28},{16,0},{20,4},{24,8},{28,12},{1,17},{... | collective-permute-start | bytes 344072 | tf_op jit(solution)/shard_map/ppermute | solution.py:371
  57.7 6.1 %collective-permute-start.24 = (bf16[64,896]{1,0:T(8,128)(2,1)S(1)}, bf16[64,896]{1,0:T(8,128)(2,1)S(1)}, u32[]{:S(2)}, u32[]{:S(2)}) collective-permute-start(bf16[64,896]{1,0:T(8,128)(2,1)S(1)} %fusion.3.refs_3_), channel_id=1, source_target_pairs={{0,24},{4,28},{8,16},{12,20},{16,8},{20,12},{24,0},{28,4},{1,25},{... | collective-permute-start | bytes 344072 | tf_op jit(solution)/shard_map/ppermute | solution.py:371
  59.3 11.7 %collective-permute-start.26 = (bf16[64,896]{1,0:T(8,128)(2,1)S(1)}, bf16[64,896]{1,0:T(8,128)(2,1)S(1)}, u32[]{:S(2)}, u32[]{:S(2)}) collective-permute-start(bf16[64,896]{1,0:T(8,128)(2,1)S(1)} %fusion.3.refs_3_), channel_id=1, source_target_pairs={{0,4},{4,0},{8,12},{12,8},{16,20},{20,16},{24,28},{28,24},{1,5},{5... | collective-permute-start | bytes 344072 | tf_op jit(solution)/shard_map/ppermute | solution.py:371
  61.7 13.4 %collective-permute-start.21 = (bf16[64,896]{1,0:T(8,128)(2,1)S(1)}, bf16[64,896]{1,0:T(8,128)(2,1)S(1)}, u32[]{:S(2)}, u32[]{:S(2)}) collective-permute-start(bf16[64,896]{1,0:T(8,128)(2,1)S(1)} %collective-permute-done.20.refs_3_), channel_id=1, source_target_pairs={{0,4},{4,0},{8,12},{12,8},{16,20},{20,16},{24,28},{28,24},{1,5},{5... | collective-permute-start | bytes 344072 | tf_op jit(solution)/shard_map/ppermute | solution.py:371
  62.5 12.6 %collective-permute-start.23 = (bf16[64,896]{1,0:T(8,128)(2,1)S(1)}, bf16[64,896]{1,0:T(8,128)(2,1)S(1)}, u32[]{:S(2)}, u32[]{:S(2)}) collective-permute-start(bf16[64,896]{1,0:T(8,128)(2,1)S(1)} %collective-permute-done.22.refs_4_), channel_id=1, source_target_pairs={{0,4},{4,0},{8,12},{12,8},{16,20},{20,16},{24,28},{28,24},{1,5},{5... | collective-permute-start | bytes 344072 | tf_op jit(solution)/shard_map/ppermute | solution.py:371
  63.8 11.4 %collective-permute-start.25 = (bf16[64,896]{1,0:T(8,128)(2,1)S(1)}, bf16[64,896]{1,0:T(8,128)(2,1)S(1)}, u32[]{:S(2)}, u32[]{:S(2)}) collective-permute-start(bf16[64,896]{1,0:T(8,128)(2,1)S(1)} %collective-permute-done.24.refs_5_), channel_id=1, source_target_pairs={{0,4},{4,0},{8,12},{12,8},{16,20},{20,16},{24,28},{28,24},{1,5},{5... | collective-permute-start | bytes 344072 | tf_op jit(solution)/shard_map/ppermute | solution.py:371
  77.7 5.3 %collective-permute-start.28 = (bf16[192,256]{1,0:T(8,128)(2,1)S(1)}, bf16[192,256]{1,0:T(8,128)(2,1)S(1)}, u32[]{:S(2)}, u32[]{:S(2)}) collective-permute-start(bf16[192,256]{1,0:T(8,128)(2,1)S(1)} %shard_map.112.h_ref), channel_id=1, source_target_pairs={{0,8},{4,12},{8,0},{12,4},{16,24},{20,28},{24,16},{28,20},{1,9},{5... | collective-permute-start | bytes 294920 | tf_op jit(solution)/shard_map/ppermute | solution.py:371
  79.5 6.7 %collective-permute-start.30 = (bf16[192,256]{1,0:T(8,128)(2,1)S(1)}, bf16[192,256]{1,0:T(8,128)(2,1)S(1)}, u32[]{:S(2)}, u32[]{:S(2)}) collective-permute-start(bf16[192,256]{1,0:T(8,128)(2,1)S(1)} %shard_map.112.h_ref), channel_id=1, source_target_pairs={{0,16},{4,20},{8,24},{12,28},{16,0},{20,4},{24,8},{28,12},{1,17},{... | collective-permute-start | bytes 294920 | tf_op jit(solution)/shard_map/ppermute | solution.py:371
  80.6 5.7 %collective-permute-start.32 = (bf16[192,256]{1,0:T(8,128)(2,1)S(1)}, bf16[192,256]{1,0:T(8,128)(2,1)S(1)}, u32[]{:S(2)}, u32[]{:S(2)}) collective-permute-start(bf16[192,256]{1,0:T(8,128)(2,1)S(1)} %shard_map.112.h_ref), channel_id=1, source_target_pairs={{0,24},{4,28},{8,16},{12,20},{16,8},{20,12},{24,0},{28,4},{1,25},{... | collective-permute-start | bytes 294920 | tf_op jit(solution)/shard_map/ppermute | solution.py:371
  81.2 11.2 %collective-permute-start.27 = (bf16[192,256]{1,0:T(8,128)(2,1)S(1)}, bf16[192,256]{1,0:T(8,128)(2,1)S(1)}, u32[]{:S(2)}, u32[]{:S(2)}) collective-permute-start(bf16[192,256]{1,0:T(8,128)(2,1)S(1)} %shard_map.112.h_ref), channel_id=1, source_target_pairs={{0,4},{4,0},{8,12},{12,8},{16,20},{20,16},{24,28},{28,24},{1,5},{5... | collective-permute-start | bytes 294920 | tf_op jit(solution)/shard_map/ppermute | solution.py:371
  82.9 9.5 %collective-permute-start.29 = (bf16[192,256]{1,0:T(8,128)(2,1)S(1)}, bf16[192,256]{1,0:T(8,128)(2,1)S(1)}, u32[]{:S(2)}, u32[]{:S(2)}) collective-permute-start(bf16[192,256]{1,0:T(8,128)(2,1)S(1)} %collective-permute-done.28.refs_1_), channel_id=1, source_target_pairs={{0,4},{4,0},{8,12},{12,8},{16,20},{20,16},{24,28},{28,24},{1,5},{5... | collective-permute-start | bytes 294920 | tf_op jit(solution)/shard_map/ppermute | solution.py:371
  86.3 6.1 %collective-permute-start.31 = (bf16[192,256]{1,0:T(8,128)(2,1)S(1)}, bf16[192,256]{1,0:T(8,128)(2,1)S(1)}, u32[]{:S(2)}, u32[]{:S(2)}) collective-permute-start(bf16[192,256]{1,0:T(8,128)(2,1)S(1)} %collective-permute-done.30.refs_2_), channel_id=1, source_target_pairs={{0,4},{4,0},{8,12},{12,8},{16,20},{20,16},{24,28},{28,24},{1,5},{5... | collective-permute-start | bytes 294920 | tf_op jit(solution)/shard_map/ppermute | solution.py:371
  86.3 6.1 %collective-permute-start.33 = (bf16[192,256]{1,0:T(8,128)(2,1)S(1)}, bf16[192,256]{1,0:T(8,128)(2,1)S(1)}, u32[]{:S(2)}, u32[]{:S(2)}) collective-permute-start(bf16[192,256]{1,0:T(8,128)(2,1)S(1)} %collective-permute-done.32.refs_3_), channel_id=1, source_target_pairs={{0,4},{4,0},{8,12},{12,8},{16,20},{20,16},{24,28},{28,24},{1,5},{5... | collective-permute-start | bytes 294920 | tf_op jit(solution)/shard_map/ppermute | solution.py:371
  94.2 4.5 %collective-permute-start.34 = (bf16[16,896]{1,0:T(8,128)(2,1)S(1)}, bf16[16,896]{1,0:T(8,128)(2,1)S(1)}, u32[]{:S(2)}, u32[]{:S(2)}) collective-permute-start(bf16[16,896]{1,0:T(8,128)(2,1)S(1)} %get-tuple-element.48), channel_id=1, source_target_pairs={{0,1},{1,0},{2,3},{3,2},{4,5},{5,4},{6,7},{7,6},{8,9},{9,8},{10,11... | collective-permute-start | bytes 86024 | tf_op jit(solution)/shard_map/ppermute | solution.py:371
  95.6 5.6 %collective-permute-start.35 = (bf16[16,896]{1,0:T(8,128)(2,1)S(1)}, bf16[16,896]{1,0:T(8,128)(2,1)S(1)}, u32[]{:S(2)}, u32[]{:S(2)}) collective-permute-start(bf16[16,896]{1,0:T(8,128)(2,1)S(1)} %get-tuple-element.50), channel_id=1, source_target_pairs={{0,2},{1,3},{2,0},{3,1},{4,6},{5,7},{6,4},{7,5},{8,10},{9,11},{10,... | collective-permute-start | bytes 86024 | tf_op jit(solution)/shard_map/ppermute | solution.py:371
  96.8 5.7 %collective-permute-start.36 = (bf16[16,896]{1,0:T(8,128)(2,1)S(1)}, bf16[16,896]{1,0:T(8,128)(2,1)S(1)}, u32[]{:S(2)}, u32[]{:S(2)}) collective-permute-start(bf16[16,896]{1,0:T(8,128)(2,1)S(1)} %get-tuple-element.49), channel_id=1, source_target_pairs={{0,3},{1,2},{2,1},{3,0},{4,7},{5,6},{6,5},{7,4},{8,11},{9,10},{10,... | collective-permute-start | bytes 86024 | tf_op jit(solution)/shard_map/ppermute | solution.py:371

commit v2 on v1

--- a/solution.py
+++ b/solution.py
@@ -398,7 +398,7 @@
     late = tuple(k + 1 for k in same)
     payload = pack(tokens, combine_num)
     gathered = [payload]
-    ups = early(payload, up_weight, same, width)
+    ups = early(payload, up_weight, same + late[:2], width)
     for k in range(1, groups):
         gathered.append(xor_permute(payload, "dp", groups, k))
     gathered = jnp.concatenate(gathered, axis=0)
@@ -436,7 +436,9 @@
         dims = (sizes, units, width, shards)
         finish = (mask, number)
         if layer == 0:
-            *sums, ups = gate_up(layer, same[1:], gates, ups, gains, xs, sums, None, *dims, load=up_weight, fill=late)
+            *sums, ups = gate_up(
+                layer, same[1:], gates, ups, gains, xs, sums, None, *dims, load=up_weight, fill=late[2:]
+            )
             (hidden,) = gate_up(layer, late, gates, ups, gains, xs, sums, finish, *dims)
         else:
             sums = gate_up(layer, (0, 1), gates, ups, gains, xs, None, None, *dims)
@@ -528,7 +530,7 @@
     fits = (
         groups & (groups - 1) == 0
         and shards & (shards - 1) == 0
-        and 4 <= shards <= widest
+        and shards == widest
         and width % lanes == 0
         and units % lanes == 0
         and rows % 16 == 0

time: 103 us -> 103 us (level)
  transfers between devices with their start and end apart: 37 -> 37, of which waited for: 15 -> 14; matrix products, arithmetic and copies ran while one was open for 0% -> 0% of each run, Pallas kernels for 31% -> 32%
where the time goes in v2:
time: 103 us
  Pallas kernels  42.9 us (42%)
  starting transfers between devices  29.4 us (29%)
  waiting for transfers between devices  29.1 us (28%)
    ppermute x37, starting transfers between devices, xor_permute(): return lax.ppermute(value, axis, [(i, i ^ bits) for i in range(size)])  29.4 us
    ppermute x37, waiting for transfers between devices, xor_permute(): return lax.ppermute(value, axis, [(i, i ^ bits) for i in range(size)])  29.1 us
    pallas_call x5, Pallas kernels, gate_up(): pl.pallas_call(functools.partial(gate_part, layer=layer, ks=ks, first=sum...  12.3 us
    pallas_call x2, Pallas kernels, down_first(): pl.pallas_call(functools.partial(down_first_kernel, layer=layer, shards=s...  8.7 us
    pallas_call x1, Pallas kernels, prefetch(): pl.pallas_call(functools.partial(prefetch_kernel, layer=layer, count=len(...  7.28 us
    pallas_call x4, Pallas kernels, down(): pl.pallas_call(functools.partial(down_part, ks=ks, first=sums is None, la...  6.01 us
    pallas_call x1, Pallas kernels, fast_device(): mask, gains, gates, *sums = prepare(stream, ups, *small)  4.36 us
    pallas_call x1, Pallas kernels, early(): pl.pallas_call(functools.partial(early_kernel, ks=ks, width=width), out_s...  3.47 us
  transfers between devices with their start and end apart: 37, of which 14 were waited for; matrix products, arithmetic and copies ran while one was open for 0% of the time, Pallas kernels for 32%

profile of v2, /device:TPU:0, one launch (start us, length us, event | category | flops | bytes accessed | tf_op | source)
XLA Modules:
  0.0 103.2 jit_solution(8002099804123693942)
XLA Ops:
  0.6 0.8 pack.1._
  1.4 3.1 %collective-permute-start = (bf16[16,1024]{1,0:T(8,128)(2,1)S(1)}, bf16[16,1024]{1,0:T(8,128)(2,1)S(1)}, u32[]{:S(2)}, u32[]{:S(2)}) collective-permute-start(bf16[16,1024]{1,0:T(8,128)(2,1)S(1)} %pack.1._), channel_id=1, source_target_pairs={{0,1},{1,0},{2,3},{3,2},{4,5},{5,4},{6,7},{7,6},{8,9},{9,8},{10,11... | collective-permute-start | bytes 98312 | tf_op jit(solution)/shard_map/ppermute | solution.py:371
  4.5 2.6 %collective-permute-start.1 = (bf16[16,1024]{1,0:T(8,128)(2,1)S(1)}, bf16[16,1024]{1,0:T(8,128)(2,1)S(1)}, u32[]{:S(2)}, u32[]{:S(2)}) collective-permute-start(bf16[16,1024]{1,0:T(8,128)(2,1)S(1)} %pack.1._), channel_id=1, source_target_pairs={{0,2},{1,3},{2,0},{3,1},{4,6},{5,7},{6,4},{7,5},{8,10},{9,11},{10,... | collective-permute-start | bytes 98312 | tf_op jit(solution)/shard_map/ppermute | solution.py:371
  7.1 3.5 %early.1.ups_ref.refs_1_ = bf16[3,256,7168]{2,1,0:T(8,128)(2,1)S(1)} custom-call(bf16[16,1024]{1,0:T(8,128)(2,1)S(1)} %pack.1._, bf16[2,3,256,7168]{3,2,1,0:T(8,128)(2,1)} %refs_2_.1), custom_call_target="tpu_custom_call" | custom-call | flops 4000000000 | bytes 20000000 | tf_op jit(solution)/shard_map/early/pallas_call | solution.py:112
  10.6 2.2 %collective-permute-done.2 = bf16[16,1024]{1,0:T(8,128)(2,1)S(1)} collective-permute-done((bf16[16,1024]{1,0:T(8,128)(2,1)S(1)}, bf16[16,1024]{1,0:T(8,128)(2,1)S(1)}, u32[]{:S(2)}, u32[]{:S(2)}) %collective-permute-start.2) | collective-permute-done | bytes 32800 | tf_op jit(solution)/shard_map/ppermute | solution.py:371
  12.9 1.6 %collective-permute-start.3 = (bf16[64,896]{1,0:T(8,128)(2,1)S(1)}, bf16[64,896]{1,0:T(8,128)(2,1)S(1)}, u32[]{:S(2)}, u32[]{:S(2)}) collective-permute-start(bf16[64,896]{1,0:T(8,128)(2,1)S(1)} %slice.72.x_ref), channel_id=1, source_target_pairs={{0,8},{4,12},{8,0},{12,4},{16,24},{20,28},{24,16},{28,20},{1,9},{5... | collective-permute-start | bytes 344072 | tf_op jit(solution)/shard_map/ppermute | solution.py:371
  14.4 1.5 %collective-permute-start.4 = (bf16[64,896]{1,0:T(8,128)(2,1)S(1)}, bf16[64,896]{1,0:T(8,128)(2,1)S(1)}, u32[]{:S(2)}, u32[]{:S(2)}) collective-permute-start(bf16[64,896]{1,0:T(8,128)(2,1)S(1)} %slice.72.x_ref), channel_id=1, source_target_pairs={{0,16},{4,20},{8,24},{12,28},{16,0},{20,4},{24,8},{28,12},{1,17},{... | collective-permute-start | bytes 344072 | tf_op jit(solution)/shard_map/ppermute | solution.py:371
  16.4 4.4 %setup.1 = (f32[2,3,8,128]{3,2,1,0:T(8,128)S(1)}, f32[2,7680]{1,0:T(2,128)S(1)}, bf16[3,256,7168]{2,1,0:T(8,128)(2,1)S(1)}, f32[2,768,128]{2,1,0:T(8,128)S(1)}, f32[64,128]{1,0:T(8,128)S(1)}) custom-call(bf16[64,896]{1,0:T(8,128)(2,1)S(1)} %slice.72.x_ref, bf16[3,256,7168]{2,1,0:T(8,128)(2,1)S(1)} %early.1.ups_ref.refs_1_, s32[2,2,4]{2,1,0:T(2,128)} %bitcast.7, ...), custom_call_target="tpu_custom_call" | custom-call | flops 4000000000 | bytes 20000000 | tf_op jit(solution)/shard_map/setup/pallas_call | solution.py:432
  20.8 0.6 collective-permute-start.7
  21.9 2.4 %shard_map.104 = (f32[2,768,128]{2,1,0:T(8,128)S(1)}, f32[64,128]{1,0:T(8,128)S(1)}, bf16[3,256,7168]{2,1,0:T(8,128)(2,1)S(1)}) custom-call(bf16[3,256,7168]{2,1,0:T(8,128)(2,1)S(1)} %get-tuple-element.24.refs_0_, bf16[3,256,7168]{2,1,0:T(8,128)(2,1)S(1)} %early.1.ups_ref.refs_1_, ...), custom_call_target="tpu_custom_call", output_to_operand_aliasing={{2}: (1, {})} | custom-call | flops 528482304 | bytes 8257536 | tf_op jit(solution)/shard_map/pallas_call | solution.py:216
  24.4 3.3 %shard_map.105.h_ref = bf16[192,256]{1,0:T(8,128)(2,1)S(1)} custom-call(bf16[3,256,7168]{2,1,0:T(8,128)(2,1)S(1)} %get-tuple-element.24.refs_0_, bf16[3,256,7168]{2,1,0:T(8,128)(2,1)S(1)} %get-tuple-element.28.refs_1_, f32[2,7680]{1,0:T(2,128)S(1)} %get-tuple-element.25.refs_2_, bf16[64,896]{1,0:T(8,128)(2,1)S(1)} %collective-permute-done.6.refs_3_, ...), custom_call_target="tpu_custom_call" | custom-call | flops 704643072 | bytes 11010048 | tf_op jit(solution)/shard_map/pallas_call | solution.py:216
  27.7 1.5 %collective-permute-start.11 = (bf16[192,256]{1,0:T(8,128)(2,1)S(1)}, bf16[192,256]{1,0:T(8,128)(2,1)S(1)}, u32[]{:S(2)}, u32[]{:S(2)}) collective-permute-start(bf16[192,256]{1,0:T(8,128)(2,1)S(1)} %shard_map.105.h_ref), channel_id=1, source_target_pairs={{0,8},{4,12},{8,0},{12,4},{16,24},{20,28},{24,16},{28,20},{1,9},{5... | collective-permute-start | bytes 294920 | tf_op jit(solution)/shard_map/ppermute | solution.py:371
  29.2 1.5 %collective-permute-start.13 = (bf16[192,256]{1,0:T(8,128)(2,1)S(1)}, bf16[192,256]{1,0:T(8,128)(2,1)S(1)}, u32[]{:S(2)}, u32[]{:S(2)}) collective-permute-start(bf16[192,256]{1,0:T(8,128)(2,1)S(1)} %shard_map.105.h_ref), channel_id=1, source_target_pairs={{0,16},{4,20},{8,24},{12,28},{16,0},{20,4},{24,8},{28,12},{1,17},{... | collective-permute-start | bytes 294920 | tf_op jit(solution)/shard_map/ppermute | solution.py:371
  30.8 0.5 collective-permute-start.15
  31.3 1.4 %collective-permute-done.11.refs_1_ = bf16[192,256]{1,0:T(8,128)(2,1)S(1)} collective-permute-done((bf16[192,256]{1,0:T(8,128)(2,1)S(1)}, bf16[192,256]{1,0:T(8,128)(2,1)S(1)}, u32[]{:S(2)}, u32[]{:S(2)}) %collective-permute-start.11) | collective-permute-done | bytes 98336 | tf_op jit(solution)/shard_map/ppermute | solution.py:371
  32.7 2.2 %collective-permute-done.13.refs_2_ = bf16[192,256]{1,0:T(8,128)(2,1)S(1)} collective-permute-done((bf16[192,256]{1,0:T(8,128)(2,1)S(1)}, bf16[192,256]{1,0:T(8,128)(2,1)S(1)}, u32[]{:S(2)}, u32[]{:S(2)}) %collective-permute-start.13) | collective-permute-done | bytes 98336 | tf_op jit(solution)/shard_map/ppermute | solution.py:371
  34.9 1.3 %collective-permute-done.15.refs_3_ = bf16[192,256]{1,0:T(8,128)(2,1)S(1)} collective-permute-done((bf16[192,256]{1,0:T(8,128)(2,1)S(1)}, bf16[192,256]{1,0:T(8,128)(2,1)S(1)}, u32[]{:S(2)}, u32[]{:S(2)}) %collective-permute-start.15) | collective-permute-done | bytes 98336 | tf_op jit(solution)/shard_map/ppermute | solution.py:371
  36.3 4.3 %shard_map.106 = (bf16[3,896,2048]{2,1,0:T(8,128)(2,1)S(1)}, f32[896,128]{1,0:T(8,128)S(1)}) custom-call(bf16[192,256]{1,0:T(8,128)(2,1)S(1)} %shard_map.105.h_ref, bf16[2,3,896,2048]{3,2,1,0:T(8,128)(2,1)} %weight_hbm.7), custom_call_target="tpu_custom_call" | custom-call | flops 4000000000 | bytes 20000000 | tf_op jit(solution)/shard_map/pallas_call | solution.py:282
  40.6 1.2 %shard_map.107.refs_5_ = f32[896,128]{1,0:T(8,128)S(1)} custom-call(bf16[3,896,2048]{2,1,0:T(8,128)(2,1)S(1)} %get-tuple-element.32.refs_0_, bf16[192,256]{1,0:T(8,128)(2,1)S(1)} %collective-permute-done.11.refs_1_, bf16[192,256]{1,0:T(8,128)(2,1)S(1)} %collective-permute-done.13.refs_2_, bf16[192,256]{1,0:T(8,128)(2,1)S(1)} %collective-permute-done.15.refs_3_, ...), custom_call_target="tpu_custom_call" | custom-call | flops 264241152 | bytes 4128768 | tf_op jit(solution)/shard_map/pallas_call | solution.py:299
  41.9 1.8 %shard_map.108 = (f32[64,896]{1,0:T(8,128)S(1)}, bf16[64,896]{1,0:T(8,128)(2,1)S(1)}) custom-call(bf16[3,896,2048]{2,1,0:T(8,128)(2,1)S(1)} %get-tuple-element.32.refs_0_, bf16[192,256]{1,0:T(8,128)(2,1)S(1)} %collective-permute-done.10.refs_1_, bf16[192,256]{1,0:T(8,128)(2,1)S(1)} %collective-permute-done.12.refs_2_, ...), custom_call_target="tpu_custom_call" | custom-call | flops 352321536 | bytes 5505024 | tf_op jit(solution)/shard_map/pallas_call | solution.py:299
  43.8 1.7 %collective-permute-start.19 = (bf16[64,896]{1,0:T(8,128)(2,1)S(1)}, bf16[64,896]{1,0:T(8,128)(2,1)S(1)}, u32[]{:S(2)}, u32[]{:S(2)}) collective-permute-start(bf16[64,896]{1,0:T(8,128)(2,1)S(1)} %get-tuple-element.35.refs_0_), channel_id=1, source_target_pairs={{0,3},{1,2},{2,1},{3,0},{4,7},{5,6},{6,5},{7,4},{8,11},{9,10},{10,... | collective-permute-start | bytes 344072 | tf_op jit(solution)/shard_map/ppermute | solution.py:371
  45.5 1.8 %collective-permute-start.17 = (bf16[64,896]{1,0:T(8,128)(2,1)S(1)}, bf16[64,896]{1,0:T(8,128)(2,1)S(1)}, u32[]{:S(2)}, u32[]{:S(2)}) collective-permute-start(bf16[64,896]{1,0:T(8,128)(2,1)S(1)} %get-tuple-element.35.refs_0_), channel_id=1, source_target_pairs={{0,1},{1,0},{2,3},{3,2},{4,5},{5,4},{6,7},{7,6},{8,9},{9,8},{10,11... | collective-permute-start | bytes 344072 | tf_op jit(solution)/shard_map/ppermute | solution.py:371
  47.3 7.0 %collective-permute-done.18 = bf16[64,896]{1,0:T(8,128)(2,1)S(1)} collective-permute-done((bf16[64,896]{1,0:T(8,128)(2,1)S(1)}, bf16[64,896]{1,0:T(8,128)(2,1)S(1)}, u32[]{:S(2)}, u32[]{:S(2)}) %collective-permute-start.18) | collective-permute-done | bytes 114720 | tf_op jit(solution)/shard_map/ppermute | solution.py:371
  54.3 1.3 %collective-permute-done.17 = bf16[64,896]{1,0:T(8,128)(2,1)S(1)} collective-permute-done((bf16[64,896]{1,0:T(8,128)(2,1)S(1)}, bf16[64,896]{1,0:T(8,128)(2,1)S(1)}, u32[]{:S(2)}, u32[]{:S(2)}) %collective-permute-start.17) | collective-permute-done | bytes 114720 | tf_op jit(solution)/shard_map/ppermute | solution.py:371
  55.7 0.8 collective-permute-start.20
  56.5 1.1 %collective-permute-start.22 = (bf16[64,896]{1,0:T(8,128)(2,1)S(1)}, bf16[64,896]{1,0:T(8,128)(2,1)S(1)}, u32[]{:S(2)}, u32[]{:S(2)}) collective-permute-start(bf16[64,896]{1,0:T(8,128)(2,1)S(1)} %fusion.3.refs_3_), channel_id=1, source_target_pairs={{0,16},{4,20},{8,24},{12,28},{16,0},{20,4},{24,8},{28,12},{1,17},{... | collective-permute-start | bytes 344072 | tf_op jit(solution)/shard_map/ppermute | solution.py:371
  57.6 1.7 %collective-permute-start.24 = (bf16[64,896]{1,0:T(8,128)(2,1)S(1)}, bf16[64,896]{1,0:T(8,128)(2,1)S(1)}, u32[]{:S(2)}, u32[]{:S(2)}) collective-permute-start(bf16[64,896]{1,0:T(8,128)(2,1)S(1)} %fusion.3.refs_3_), channel_id=1, source_target_pairs={{0,24},{4,28},{8,16},{12,20},{16,8},{20,12},{24,0},{28,4},{1,25},{... | collective-permute-start | bytes 344072 | tf_op jit(solution)/shard_map/ppermute | solution.py:371
  59.3 2.4 %collective-permute-done.20.refs_3_ = bf16[64,896]{1,0:T(8,128)(2,1)S(1)} collective-permute-done((bf16[64,896]{1,0:T(8,128)(2,1)S(1)}, bf16[64,896]{1,0:T(8,128)(2,1)S(1)}, u32[]{:S(2)}, u32[]{:S(2)}) %collective-permute-start.20) | collective-permute-done | bytes 114720 | tf_op jit(solution)/shard_map/ppermute | solution.py:371
  61.7 0.7 collective-permute-done.22.refs_4_
  62.4 1.2 %collective-permute-done.24.refs_5_ = bf16[64,896]{1,0:T(8,128)(2,1)S(1)} collective-permute-done((bf16[64,896]{1,0:T(8,128)(2,1)S(1)}, bf16[64,896]{1,0:T(8,128)(2,1)S(1)}, u32[]{:S(2)}, u32[]{:S(2)}) %collective-permute-start.24) | collective-permute-done | bytes 114720 | tf_op jit(solution)/shard_map/ppermute | solution.py:371
  63.6 7.3 %shard_map.109 = (bf16[3,256,7168]{2,1,0:T(8,128)(2,1)S(1)}, bf16[3,256,7168]{2,1,0:T(8,128)(2,1)S(1)}) custom-call(bf16[64,896]{1,0:T(8,128)(2,1)S(1)} %get-tuple-element.35.refs_0_, bf16[2,3,256,7168]{3,2,1,0:T(8,128)(2,1)} %refs_1_.1, bf16[2,3,256,7168]{3,2,1,0:T(8,128)(2,1)} %refs_2_.1), custom_call_target="tpu_custom_call" | custom-call | flops 8808038400 | bytes 44040192 | tf_op jit(solution)/shard_map/pallas_call | solution.py:359
  70.9 1.8 %shard_map.110 = (f32[2,768,128]{2,1,0:T(8,128)S(1)}, f32[64,128]{1,0:T(8,128)S(1)}) custom-call(bf16[3,256,7168]{2,1,0:T(8,128)(2,1)S(1)} %get-tuple-element.36.refs_0_, bf16[3,256,7168]{2,1,0:T(8,128)(2,1)S(1)} %get-tuple-element.37.refs_1_, f32[2,7680]{1,0:T(2,128)S(1)} %get-tuple-element.25.refs_2_, bf16[64,896]{1,0:T(8,128)(2,1)S(1)} %fusion.3.refs_3_, ...), custom_call_target="tpu_custom_call" | custom-call | flops 352321536 | bytes 5505024 | tf_op jit(solution)/shard_map/pallas_call | solution.py:216
  72.7 2.3 %shard_map.111 = (f32[2,768,128]{2,1,0:T(8,128)S(1)}, f32[64,128]{1,0:T(8,128)S(1)}) custom-call(bf16[3,256,7168]{2,1,0:T(8,128)(2,1)S(1)} %get-tuple-element.36.refs_0_, bf16[3,256,7168]{2,1,0:T(8,128)(2,1)S(1)} %get-tuple-element.37.refs_1_, f32[2,7680]{1,0:T(2,128)S(1)} %get-tuple-element.25.refs_2_, bf16[64,896]{1,0:T(8,128)(2,1)S(1)} %collective-permute-done.20.refs_3_, ...), custom_call_target="tpu_custom_call" | custom-call | flops 528482304 | bytes 8257536 | tf_op jit(solution)/shard_map/pallas_call | solution.py:216
  75.0 2.4 %shard_map.112.h_ref = bf16[192,256]{1,0:T(8,128)(2,1)S(1)} custom-call(bf16[3,256,7168]{2,1,0:T(8,128)(2,1)S(1)} %get-tuple-element.36.refs_0_, bf16[3,256,7168]{2,1,0:T(8,128)(2,1)S(1)} %get-tuple-element.37.refs_1_, f32[2,7680]{1,0:T(2,128)S(1)} %get-tuple-element.25.refs_2_, bf16[64,896]{1,0:T(8,128)(2,1)S(1)} %collective-permute-done.21.refs_3_, ...), custom_call_target="tpu_custom_call" | custom-call | flops 528482304 | bytes 8257536 | tf_op jit(solution)/shard_map/pallas_call | solution.py:216
  77.5 1.9 %collective-permute-start.28 = (bf16[192,256]{1,0:T(8,128)(2,1)S(1)}, bf16[192,256]{1,0:T(8,128)(2,1)S(1)}, u32[]{:S(2)}, u32[]{:S(2)}) collective-permute-start(bf16[192,256]{1,0:T(8,128)(2,1)S(1)} %shard_map.112.h_ref), channel_id=1, source_target_pairs={{0,8},{4,12},{8,0},{12,4},{16,24},{20,28},{24,16},{28,20},{1,9},{5... | collective-permute-start | bytes 294920 | tf_op jit(solution)/shard_map/ppermute | solution.py:371
  79.4 1.1 %collective-permute-start.30 = (bf16[192,256]{1,0:T(8,128)(2,1)S(1)}, bf16[192,256]{1,0:T(8,128)(2,1)S(1)}, u32[]{:S(2)}, u32[]{:S(2)}) collective-permute-start(bf16[192,256]{1,0:T(8,128)(2,1)S(1)} %shard_map.112.h_ref), channel_id=1, source_target_pairs={{0,16},{4,20},{8,24},{12,28},{16,0},{20,4},{24,8},{28,12},{1,17},{... | collective-permute-start | bytes 294920 | tf_op jit(solution)/shard_map/ppermute | solution.py:371
  80.5 0.6 collective-permute-start.32
  81.0 1.7 %collective-permute-done.28.refs_1_ = bf16[192,256]{1,0:T(8,128)(2,1)S(1)} collective-permute-done((bf16[192,256]{1,0:T(8,128)(2,1)S(1)}, bf16[192,256]{1,0:T(8,128)(2,1)S(1)}, u32[]{:S(2)}, u32[]{:S(2)}) %collective-permute-start.28) | collective-permute-done | bytes 98336 | tf_op jit(solution)/shard_map/ppermute | solution.py:371
  82.7 3.4 %collective-permute-done.30.refs_2_ = bf16[192,256]{1,0:T(8,128)(2,1)S(1)} collective-permute-done((bf16[192,256]{1,0:T(8,128)(2,1)S(1)}, bf16[192,256]{1,0:T(8,128)(2,1)S(1)}, u32[]{:S(2)}, u32[]{:S(2)}) %collective-permute-start.30) | collective-permute-done | bytes 98336 | tf_op jit(solution)/shard_map/ppermute | solution.py:371
  86.6 4.3 %shard_map.113 = (bf16[3,896,2048]{2,1,0:T(8,128)(2,1)S(1)}, f32[896,128]{1,0:T(8,128)S(1)}) custom-call(bf16[192,256]{1,0:T(8,128)(2,1)S(1)} %shard_map.112.h_ref, bf16[2,3,896,2048]{3,2,1,0:T(8,128)(2,1)} %weight_hbm.7), custom_call_target="tpu_custom_call" | custom-call | flops 4000000000 | bytes 20000000 | tf_op jit(solution)/shard_map/pallas_call | solution.py:282
  91.0 1.2 %shard_map.114.refs_5_ = f32[896,128]{1,0:T(8,128)S(1)} custom-call(bf16[3,896,2048]{2,1,0:T(8,128)(2,1)S(1)} %get-tuple-element.42.refs_0_, bf16[192,256]{1,0:T(8,128)(2,1)S(1)} %collective-permute-done.28.refs_1_, bf16[192,256]{1,0:T(8,128)(2,1)S(1)} %collective-permute-done.30.refs_2_, bf16[192,256]{1,0:T(8,128)(2,1)S(1)} %collective-permute-done.32.refs_3_, ...), custom_call_target="tpu_custom_call" | custom-call | flops 264241152 | bytes 4128768 | tf_op jit(solution)/shard_map/pallas_call | solution.py:299
  92.3 1.8 %shard_map.115 = (f32[64,896]{1,0:T(8,128)S(1)}, bf16[64,896]{1,0:T(8,128)(2,1)S(1)}) custom-call(bf16[3,896,2048]{2,1,0:T(8,128)(2,1)S(1)} %get-tuple-element.42.refs_0_, bf16[192,256]{1,0:T(8,128)(2,1)S(1)} %collective-permute-done.27.refs_1_, bf16[192,256]{1,0:T(8,128)(2,1)S(1)} %collective-permute-done.29.refs_2_, ...), custom_call_target="tpu_custom_call" | custom-call | flops 352321536 | bytes 5505024 | tf_op jit(solution)/shard_map/pallas_call | solution.py:299
  94.0 1.9 %collective-permute-start.34 = (bf16[16,896]{1,0:T(8,128)(2,1)S(1)}, bf16[16,896]{1,0:T(8,128)(2,1)S(1)}, u32[]{:S(2)}, u32[]{:S(2)}) collective-permute-start(bf16[16,896]{1,0:T(8,128)(2,1)S(1)} %get-tuple-element.48), channel_id=1, source_target_pairs={{0,1},{1,0},{2,3},{3,2},{4,5},{5,4},{6,7},{7,6},{8,9},{9,8},{10,11... | collective-permute-start | bytes 86024 | tf_op jit(solution)/shard_map/ppermute | solution.py:371
  95.9 1.0 collective-permute-start.35
  96.9 1.6 %collective-permute-start.36 = (bf16[16,896]{1,0:T(8,128)(2,1)S(1)}, bf16[16,896]{1,0:T(8,128)(2,1)S(1)}, u32[]{:S(2)}, u32[]{:S(2)}) collective-permute-start(bf16[16,896]{1,0:T(8,128)(2,1)S(1)} %get-tuple-element.49), channel_id=1, source_target_pairs={{0,3},{1,2},{2,1},{3,0},{4,7},{5,6},{6,5},{7,4},{8,11},{9,10},{10,... | collective-permute-start | bytes 86024 | tf_op jit(solution)/shard_map/ppermute | solution.py:371
  98.5 2.8 %collective-permute-done.35 = bf16[16,896]{1,0:T(8,128)(2,1)S(1)} collective-permute-done((bf16[16,896]{1,0:T(8,128)(2,1)S(1)}, bf16[16,896]{1,0:T(8,128)(2,1)S(1)}, u32[]{:S(2)}, u32[]{:S(2)}) %collective-permute-start.35) | collective-permute-done | bytes 28704 | tf_op jit(solution)/shard_map/ppermute | solution.py:371
  101.3 1.3 %collective-permute-done.36 = bf16[16,896]{1,0:T(8,128)(2,1)S(1)} collective-permute-done((bf16[16,896]{1,0:T(8,128)(2,1)S(1)}, bf16[16,896]{1,0:T(8,128)(2,1)S(1)}, u32[]{:S(2)}, u32[]{:S(2)}) %collective-permute-start.36) | collective-permute-done | bytes 28704 | tf_op jit(solution)/shard_map/ppermute | solution.py:371
  102.5 0.6 fusion.4
  (50 shorter events, 1.8 us)
Async XLA Ops:
  1.4 9.2 %collective-permute-start = (bf16[16,1024]{1,0:T(8,128)(2,1)S(1)}, bf16[16,1024]{1,0:T(8,128)(2,1)S(1)}, u32[]{:S(2)}, u32[]{:S(2)}) collective-permute-start(bf16[16,1024]{1,0:T(8,128)(2,1)S(1)} %pack.1._), channel_id=1, source_target_pairs={{0,1},{1,0},{2,3},{3,2},{4,5},{5,4},{6,7},{7,6},{8,9},{9,8},{10,11... | collective-permute-start | bytes 98312 | tf_op jit(solution)/shard_map/ppermute | solution.py:371
  4.5 6.1 %collective-permute-start.1 = (bf16[16,1024]{1,0:T(8,128)(2,1)S(1)}, bf16[16,1024]{1,0:T(8,128)(2,1)S(1)}, u32[]{:S(2)}, u32[]{:S(2)}) collective-permute-start(bf16[16,1024]{1,0:T(8,128)(2,1)S(1)} %pack.1._), channel_id=1, source_target_pairs={{0,2},{1,3},{2,0},{3,1},{4,6},{5,7},{6,4},{7,5},{8,10},{9,11},{10,... | collective-permute-start | bytes 98312 | tf_op jit(solution)/shard_map/ppermute | solution.py:371
  7.1 5.7 %collective-permute-start.2 = (bf16[16,1024]{1,0:T(8,128)(2,1)S(1)}, bf16[16,1024]{1,0:T(8,128)(2,1)S(1)}, u32[]{:S(2)}, u32[]{:S(2)}) collective-permute-start(bf16[16,1024]{1,0:T(8,128)(2,1)S(1)} %pack.1._), channel_id=1, source_target_pairs={{0,3},{1,2},{2,1},{3,0},{4,7},{5,6},{6,5},{7,4},{8,11},{9,10},{10,... | collective-permute-start | bytes 98312 | tf_op jit(solution)/shard_map/ppermute | solution.py:371
  12.9 7.9 %collective-permute-start.3 = (bf16[64,896]{1,0:T(8,128)(2,1)S(1)}, bf16[64,896]{1,0:T(8,128)(2,1)S(1)}, u32[]{:S(2)}, u32[]{:S(2)}) collective-permute-start(bf16[64,896]{1,0:T(8,128)(2,1)S(1)} %slice.72.x_ref), channel_id=1, source_target_pairs={{0,8},{4,12},{8,0},{12,4},{16,24},{20,28},{24,16},{28,20},{1,9},{5... | collective-permute-start | bytes 344072 | tf_op jit(solution)/shard_map/ppermute | solution.py:371
  14.4 7.0 %collective-permute-start.4 = (bf16[64,896]{1,0:T(8,128)(2,1)S(1)}, bf16[64,896]{1,0:T(8,128)(2,1)S(1)}, u32[]{:S(2)}, u32[]{:S(2)}) collective-permute-start(bf16[64,896]{1,0:T(8,128)(2,1)S(1)} %slice.72.x_ref), channel_id=1, source_target_pairs={{0,16},{4,20},{8,24},{12,28},{16,0},{20,4},{24,8},{28,12},{1,17},{... | collective-permute-start | bytes 344072 | tf_op jit(solution)/shard_map/ppermute | solution.py:371
  15.9 5.7 %collective-permute-start.5 = (bf16[64,896]{1,0:T(8,128)(2,1)S(1)}, bf16[64,896]{1,0:T(8,128)(2,1)S(1)}, u32[]{:S(2)}, u32[]{:S(2)}) collective-permute-start(bf16[64,896]{1,0:T(8,128)(2,1)S(1)} %slice.72.x_ref), channel_id=1, source_target_pairs={{0,24},{4,28},{8,16},{12,20},{16,8},{20,12},{24,0},{28,4},{1,25},{... | collective-permute-start | bytes 344072 | tf_op jit(solution)/shard_map/ppermute | solution.py:371
  16.4 7.9 %collective-permute-start.6 = (bf16[64,896]{1,0:T(8,128)(2,1)S(1)}, bf16[64,896]{1,0:T(8,128)(2,1)S(1)}, u32[]{:S(2)}, u32[]{:S(2)}) collective-permute-start(bf16[64,896]{1,0:T(8,128)(2,1)S(1)} %slice.72.x_ref), channel_id=1, source_target_pairs={{0,4},{4,0},{8,12},{12,8},{16,20},{20,16},{24,28},{28,24},{1,5},{5... | collective-permute-start | bytes 344072 | tf_op jit(solution)/shard_map/ppermute | solution.py:371
  20.8 3.6 %collective-permute-start.7 = (bf16[64,896]{1,0:T(8,128)(2,1)S(1)}, bf16[64,896]{1,0:T(8,128)(2,1)S(1)}, u32[]{:S(2)}, u32[]{:S(2)}) collective-permute-start(bf16[64,896]{1,0:T(8,128)(2,1)S(1)} %collective-permute-done.3.refs_3_), channel_id=1, source_target_pairs={{0,4},{4,0},{8,12},{12,8},{16,20},{20,16},{24,28},{28,24},{1,5},{5... | collective-permute-start | bytes 344072 | tf_op jit(solution)/shard_map/ppermute | solution.py:371
  21.4 3.0 %collective-permute-start.8 = (bf16[64,896]{1,0:T(8,128)(2,1)S(1)}, bf16[64,896]{1,0:T(8,128)(2,1)S(1)}, u32[]{:S(2)}, u32[]{:S(2)}) collective-permute-start(bf16[64,896]{1,0:T(8,128)(2,1)S(1)} %collective-permute-done.4.refs_4_), channel_id=1, source_target_pairs={{0,4},{4,0},{8,12},{12,8},{16,20},{20,16},{24,28},{28,24},{1,5},{5... | collective-permute-start | bytes 344072 | tf_op jit(solution)/shard_map/ppermute | solution.py:371
  21.6 2.7 %collective-permute-start.9 = (bf16[64,896]{1,0:T(8,128)(2,1)S(1)}, bf16[64,896]{1,0:T(8,128)(2,1)S(1)}, u32[]{:S(2)}, u32[]{:S(2)}) collective-permute-start(bf16[64,896]{1,0:T(8,128)(2,1)S(1)} %collective-permute-done.5.refs_5_), channel_id=1, source_target_pairs={{0,4},{4,0},{8,12},{12,8},{16,20},{20,16},{24,28},{28,24},{1,5},{5... | collective-permute-start | bytes 344072 | tf_op jit(solution)/shard_map/ppermute | solution.py:371
  27.7 5.0 %collective-permute-start.11 = (bf16[192,256]{1,0:T(8,128)(2,1)S(1)}, bf16[192,256]{1,0:T(8,128)(2,1)S(1)}, u32[]{:S(2)}, u32[]{:S(2)}) collective-permute-start(bf16[192,256]{1,0:T(8,128)(2,1)S(1)} %shard_map.105.h_ref), channel_id=1, source_target_pairs={{0,8},{4,12},{8,0},{12,4},{16,24},{20,28},{24,16},{28,20},{1,9},{5... | collective-permute-start | bytes 294920 | tf_op jit(solution)/shard_map/ppermute | solution.py:371
  29.2 5.7 %collective-permute-start.13 = (bf16[192,256]{1,0:T(8,128)(2,1)S(1)}, bf16[192,256]{1,0:T(8,128)(2,1)S(1)}, u32[]{:S(2)}, u32[]{:S(2)}) collective-permute-start(bf16[192,256]{1,0:T(8,128)(2,1)S(1)} %shard_map.105.h_ref), channel_id=1, source_target_pairs={{0,16},{4,20},{8,24},{12,28},{16,0},{20,4},{24,8},{28,12},{1,17},{... | collective-permute-start | bytes 294920 | tf_op jit(solution)/shard_map/ppermute | solution.py:371
  30.8 5.5 %collective-permute-start.15 = (bf16[192,256]{1,0:T(8,128)(2,1)S(1)}, bf16[192,256]{1,0:T(8,128)(2,1)S(1)}, u32[]{:S(2)}, u32[]{:S(2)}) collective-permute-start(bf16[192,256]{1,0:T(8,128)(2,1)S(1)} %shard_map.105.h_ref), channel_id=1, source_target_pairs={{0,24},{4,28},{8,16},{12,20},{16,8},{20,12},{24,0},{28,4},{1,25},{... | collective-permute-start | bytes 294920 | tf_op jit(solution)/shard_map/ppermute | solution.py:371
  31.3 10.6 %collective-permute-start.10 = (bf16[192,256]{1,0:T(8,128)(2,1)S(1)}, bf16[192,256]{1,0:T(8,128)(2,1)S(1)}, u32[]{:S(2)}, u32[]{:S(2)}) collective-permute-start(bf16[192,256]{1,0:T(8,128)(2,1)S(1)} %shard_map.105.h_ref), channel_id=1, source_target_pairs={{0,4},{4,0},{8,12},{12,8},{16,20},{20,16},{24,28},{28,24},{1,5},{5... | collective-permute-start | bytes 294920 | tf_op jit(solution)/shard_map/ppermute | solution.py:371
  32.7 9.2 %collective-permute-start.12 = (bf16[192,256]{1,0:T(8,128)(2,1)S(1)}, bf16[192,256]{1,0:T(8,128)(2,1)S(1)}, u32[]{:S(2)}, u32[]{:S(2)}) collective-permute-start(bf16[192,256]{1,0:T(8,128)(2,1)S(1)} %collective-permute-done.11.refs_1_), channel_id=1, source_target_pairs={{0,4},{4,0},{8,12},{12,8},{16,20},{20,16},{24,28},{28,24},{1,5},{5... | collective-permute-start | bytes 294920 | tf_op jit(solution)/shard_map/ppermute | solution.py:371
  34.9 7.0 %collective-permute-start.14 = (bf16[192,256]{1,0:T(8,128)(2,1)S(1)}, bf16[192,256]{1,0:T(8,128)(2,1)S(1)}, u32[]{:S(2)}, u32[]{:S(2)}) collective-permute-start(bf16[192,256]{1,0:T(8,128)(2,1)S(1)} %collective-permute-done.13.refs_2_), channel_id=1, source_target_pairs={{0,4},{4,0},{8,12},{12,8},{16,20},{20,16},{24,28},{28,24},{1,5},{5... | collective-permute-start | bytes 294920 | tf_op jit(solution)/shard_map/ppermute | solution.py:371
  36.3 5.6 %collective-permute-start.16 = (bf16[192,256]{1,0:T(8,128)(2,1)S(1)}, bf16[192,256]{1,0:T(8,128)(2,1)S(1)}, u32[]{:S(2)}, u32[]{:S(2)}) collective-permute-start(bf16[192,256]{1,0:T(8,128)(2,1)S(1)} %collective-permute-done.15.refs_3_), channel_id=1, source_target_pairs={{0,4},{4,0},{8,12},{12,8},{16,20},{20,16},{24,28},{28,24},{1,5},{5... | collective-permute-start | bytes 294920 | tf_op jit(solution)/shard_map/ppermute | solution.py:371
  43.7 10.5 %collective-permute-start.18 = (bf16[64,896]{1,0:T(8,128)(2,1)S(1)}, bf16[64,896]{1,0:T(8,128)(2,1)S(1)}, u32[]{:S(2)}, u32[]{:S(2)}) collective-permute-start(bf16[64,896]{1,0:T(8,128)(2,1)S(1)} %get-tuple-element.35.refs_0_), channel_id=1, source_target_pairs={{0,2},{1,3},{2,0},{3,1},{4,6},{5,7},{6,4},{7,5},{8,10},{9,11},{10,... | collective-permute-start | bytes 344072 | tf_op jit(solution)/shard_map/ppermute | solution.py:371
  43.8 10.5 %collective-permute-start.19 = (bf16[64,896]{1,0:T(8,128)(2,1)S(1)}, bf16[64,896]{1,0:T(8,128)(2,1)S(1)}, u32[]{:S(2)}, u32[]{:S(2)}) collective-permute-start(bf16[64,896]{1,0:T(8,128)(2,1)S(1)} %get-tuple-element.35.refs_0_), channel_id=1, source_target_pairs={{0,3},{1,2},{2,1},{3,0},{4,7},{5,6},{6,5},{7,4},{8,11},{9,10},{10,... | collective-permute-start | bytes 344072 | tf_op jit(solution)/shard_map/ppermute | solution.py:371
  45.5 10.1 %collective-permute-start.17 = (bf16[64,896]{1,0:T(8,128)(2,1)S(1)}, bf16[64,896]{1,0:T(8,128)(2,1)S(1)}, u32[]{:S(2)}, u32[]{:S(2)}) collective-permute-start(bf16[64,896]{1,0:T(8,128)(2,1)S(1)} %get-tuple-element.35.refs_0_), channel_id=1, source_target_pairs={{0,1},{1,0},{2,3},{3,2},{4,5},{5,4},{6,7},{7,6},{8,9},{9,8},{10,11... | collective-permute-start | bytes 344072 | tf_op jit(solution)/shard_map/ppermute | solution.py:371
  55.7 6.0 %collective-permute-start.20 = (bf16[64,896]{1,0:T(8,128)(2,1)S(1)}, bf16[64,896]{1,0:T(8,128)(2,1)S(1)}, u32[]{:S(2)}, u32[]{:S(2)}) collective-permute-start(bf16[64,896]{1,0:T(8,128)(2,1)S(1)} %fusion.3.refs_3_), channel_id=1, source_target_pairs={{0,8},{4,12},{8,0},{12,4},{16,24},{20,28},{24,16},{28,20},{1,9},{5... | collective-permute-start | bytes 344072 | tf_op jit(solution)/shard_map/ppermute | solution.py:371
  56.5 5.8 %collective-permute-start.22 = (bf16[64,896]{1,0:T(8,128)(2,1)S(1)}, bf16[64,896]{1,0:T(8,128)(2,1)S(1)}, u32[]{:S(2)}, u32[]{:S(2)}) collective-permute-start(bf16[64,896]{1,0:T(8,128)(2,1)S(1)} %fusion.3.refs_3_), channel_id=1, source_target_pairs={{0,16},{4,20},{8,24},{12,28},{16,0},{20,4},{24,8},{28,12},{1,17},{... | collective-permute-start | bytes 344072 | tf_op jit(solution)/shard_map/ppermute | solution.py:371
  57.6 6.0 %collective-permute-start.24 = (bf16[64,896]{1,0:T(8,128)(2,1)S(1)}, bf16[64,896]{1,0:T(8,128)(2,1)S(1)}, u32[]{:S(2)}, u32[]{:S(2)}) collective-permute-start(bf16[64,896]{1,0:T(8,128)(2,1)S(1)} %fusion.3.refs_3_), channel_id=1, source_target_pairs={{0,24},{4,28},{8,16},{12,20},{16,8},{20,12},{24,0},{28,4},{1,25},{... | collective-permute-start | bytes 344072 | tf_op jit(solution)/shard_map/ppermute | solution.py:371
  59.3 11.6 %collective-permute-start.26 = (bf16[64,896]{1,0:T(8,128)(2,1)S(1)}, bf16[64,896]{1,0:T(8,128)(2,1)S(1)}, u32[]{:S(2)}, u32[]{:S(2)}) collective-permute-start(bf16[64,896]{1,0:T(8,128)(2,1)S(1)} %fusion.3.refs_3_), channel_id=1, source_target_pairs={{0,4},{4,0},{8,12},{12,8},{16,20},{20,16},{24,28},{28,24},{1,5},{5... | collective-permute-start | bytes 344072 | tf_op jit(solution)/shard_map/ppermute | solution.py:371
  61.7 13.3 %collective-permute-start.21 = (bf16[64,896]{1,0:T(8,128)(2,1)S(1)}, bf16[64,896]{1,0:T(8,128)(2,1)S(1)}, u32[]{:S(2)}, u32[]{:S(2)}) collective-permute-start(bf16[64,896]{1,0:T(8,128)(2,1)S(1)} %collective-permute-done.20.refs_3_), channel_id=1, source_target_pairs={{0,4},{4,0},{8,12},{12,8},{16,20},{20,16},{24,28},{28,24},{1,5},{5... | collective-permute-start | bytes 344072 | tf_op jit(solution)/shard_map/ppermute | solution.py:371
  62.4 12.6 %collective-permute-start.23 = (bf16[64,896]{1,0:T(8,128)(2,1)S(1)}, bf16[64,896]{1,0:T(8,128)(2,1)S(1)}, u32[]{:S(2)}, u32[]{:S(2)}) collective-permute-start(bf16[64,896]{1,0:T(8,128)(2,1)S(1)} %collective-permute-done.22.refs_4_), channel_id=1, source_target_pairs={{0,4},{4,0},{8,12},{12,8},{16,20},{20,16},{24,28},{28,24},{1,5},{5... | collective-permute-start | bytes 344072 | tf_op jit(solution)/shard_map/ppermute | solution.py:371
  63.6 11.4 %collective-permute-start.25 = (bf16[64,896]{1,0:T(8,128)(2,1)S(1)}, bf16[64,896]{1,0:T(8,128)(2,1)S(1)}, u32[]{:S(2)}, u32[]{:S(2)}) collective-permute-start(bf16[64,896]{1,0:T(8,128)(2,1)S(1)} %collective-permute-done.24.refs_5_), channel_id=1, source_target_pairs={{0,4},{4,0},{8,12},{12,8},{16,20},{20,16},{24,28},{28,24},{1,5},{5... | collective-permute-start | bytes 344072 | tf_op jit(solution)/shard_map/ppermute | solution.py:371
  77.5 5.3 %collective-permute-start.28 = (bf16[192,256]{1,0:T(8,128)(2,1)S(1)}, bf16[192,256]{1,0:T(8,128)(2,1)S(1)}, u32[]{:S(2)}, u32[]{:S(2)}) collective-permute-start(bf16[192,256]{1,0:T(8,128)(2,1)S(1)} %shard_map.112.h_ref), channel_id=1, source_target_pairs={{0,8},{4,12},{8,0},{12,4},{16,24},{20,28},{24,16},{28,20},{1,9},{5... | collective-permute-start | bytes 294920 | tf_op jit(solution)/shard_map/ppermute | solution.py:371
  79.4 6.7 %collective-permute-start.30 = (bf16[192,256]{1,0:T(8,128)(2,1)S(1)}, bf16[192,256]{1,0:T(8,128)(2,1)S(1)}, u32[]{:S(2)}, u32[]{:S(2)}) collective-permute-start(bf16[192,256]{1,0:T(8,128)(2,1)S(1)} %shard_map.112.h_ref), channel_id=1, source_target_pairs={{0,16},{4,20},{8,24},{12,28},{16,0},{20,4},{24,8},{28,12},{1,17},{... | collective-permute-start | bytes 294920 | tf_op jit(solution)/shard_map/ppermute | solution.py:371
  80.5 5.6 %collective-permute-start.32 = (bf16[192,256]{1,0:T(8,128)(2,1)S(1)}, bf16[192,256]{1,0:T(8,128)(2,1)S(1)}, u32[]{:S(2)}, u32[]{:S(2)}) collective-permute-start(bf16[192,256]{1,0:T(8,128)(2,1)S(1)} %shard_map.112.h_ref), channel_id=1, source_target_pairs={{0,24},{4,28},{8,16},{12,20},{16,8},{20,12},{24,0},{28,4},{1,25},{... | collective-permute-start | bytes 294920 | tf_op jit(solution)/shard_map/ppermute | solution.py:371
  81.0 11.2 %collective-permute-start.27 = (bf16[192,256]{1,0:T(8,128)(2,1)S(1)}, bf16[192,256]{1,0:T(8,128)(2,1)S(1)}, u32[]{:S(2)}, u32[]{:S(2)}) collective-permute-start(bf16[192,256]{1,0:T(8,128)(2,1)S(1)} %shard_map.112.h_ref), channel_id=1, source_target_pairs={{0,4},{4,0},{8,12},{12,8},{16,20},{20,16},{24,28},{28,24},{1,5},{5... | collective-permute-start | bytes 294920 | tf_op jit(solution)/shard_map/ppermute | solution.py:371
  82.7 9.5 %collective-permute-start.29 = (bf16[192,256]{1,0:T(8,128)(2,1)S(1)}, bf16[192,256]{1,0:T(8,128)(2,1)S(1)}, u32[]{:S(2)}, u32[]{:S(2)}) collective-permute-start(bf16[192,256]{1,0:T(8,128)(2,1)S(1)} %collective-permute-done.28.refs_1_), channel_id=1, source_target_pairs={{0,4},{4,0},{8,12},{12,8},{16,20},{20,16},{24,28},{28,24},{1,5},{5... | collective-permute-start | bytes 294920 | tf_op jit(solution)/shard_map/ppermute | solution.py:371
  86.1 6.1 %collective-permute-start.31 = (bf16[192,256]{1,0:T(8,128)(2,1)S(1)}, bf16[192,256]{1,0:T(8,128)(2,1)S(1)}, u32[]{:S(2)}, u32[]{:S(2)}) collective-permute-start(bf16[192,256]{1,0:T(8,128)(2,1)S(1)} %collective-permute-done.30.refs_2_), channel_id=1, source_target_pairs={{0,4},{4,0},{8,12},{12,8},{16,20},{20,16},{24,28},{28,24},{1,5},{5... | collective-permute-start | bytes 294920 | tf_op jit(solution)/shard_map/ppermute | solution.py:371
  86.1 6.1 %collective-permute-start.33 = (bf16[192,256]{1,0:T(8,128)(2,1)S(1)}, bf16[192,256]{1,0:T(8,128)(2,1)S(1)}, u32[]{:S(2)}, u32[]{:S(2)}) collective-permute-start(bf16[192,256]{1,0:T(8,128)(2,1)S(1)} %collective-permute-done.32.refs_3_), channel_id=1, source_target_pairs={{0,4},{4,0},{8,12},{12,8},{16,20},{20,16},{24,28},{28,24},{1,5},{5... | collective-permute-start | bytes 294920 | tf_op jit(solution)/shard_map/ppermute | solution.py:371
  94.0 4.5 %collective-permute-start.34 = (bf16[16,896]{1,0:T(8,128)(2,1)S(1)}, bf16[16,896]{1,0:T(8,128)(2,1)S(1)}, u32[]{:S(2)}, u32[]{:S(2)}) collective-permute-start(bf16[16,896]{1,0:T(8,128)(2,1)S(1)} %get-tuple-element.48), channel_id=1, source_target_pairs={{0,1},{1,0},{2,3},{3,2},{4,5},{5,4},{6,7},{7,6},{8,9},{9,8},{10,11... | collective-permute-start | bytes 86024 | tf_op jit(solution)/shard_map/ppermute | solution.py:371
  95.9 5.4 %collective-permute-start.35 = (bf16[16,896]{1,0:T(8,128)(2,1)S(1)}, bf16[16,896]{1,0:T(8,128)(2,1)S(1)}, u32[]{:S(2)}, u32[]{:S(2)}) collective-permute-start(bf16[16,896]{1,0:T(8,128)(2,1)S(1)} %get-tuple-element.50), channel_id=1, source_target_pairs={{0,2},{1,3},{2,0},{3,1},{4,6},{5,7},{6,4},{7,5},{8,10},{9,11},{10,... | collective-permute-start | bytes 86024 | tf_op jit(solution)/shard_map/ppermute | solution.py:371
  96.9 5.7 %collective-permute-start.36 = (bf16[16,896]{1,0:T(8,128)(2,1)S(1)}, bf16[16,896]{1,0:T(8,128)(2,1)S(1)}, u32[]{:S(2)}, u32[]{:S(2)}) collective-permute-start(bf16[16,896]{1,0:T(8,128)(2,1)S(1)} %get-tuple-element.49), channel_id=1, source_target_pairs={{0,3},{1,2},{2,1},{3,0},{4,7},{5,6},{6,5},{7,4},{8,11},{9,10},{10,... | collective-permute-start | bytes 86024 | tf_op jit(solution)/shard_map/ppermute | solution.py:371
